TPU v7x, 32 devices: a whole 2x2x4 slice. The times are simulated.
32 devices in a mesh: groups: 2 (over y), expert: 8 (over z, x), tensor: 2 (over core).
Axes of the slice: x: 2, y: 2, z: 4, core: 2. Of those that a mesh axis runs over, the one named last changes fastest.
Arguments:
- tokens: bfloat16 [1024, 1536], P(('groups', 'expert')), parts along dimension 0, may hold values from -12 to 12
- gain: float32 [1536], replicated, may hold values from 0.25 to 1.75
- route_ids: int32 [1024, 4], P(('groups', 'expert')), parts along dimension 0, may hold values from 0 to 3, as said below
- route_weights: float32 [1024, 4], P(('groups', 'expert')), parts along dimension 0, may hold values from 0.05 to 0.5
- w_gate: bfloat16 [8, 1536, 768], P('expert', None, 'tensor'), may hold values from -0.15625 to 0.15625
- w_up: bfloat16 [8, 1536, 768], P('expert', None, 'tensor'), may hold values from -0.15625 to 0.15625
- w_down: bfloat16 [8, 768, 1536], P('expert', 'tensor'), may hold values from -0.15625 to 0.15625
Outputs:
- mixed: bfloat16 [1024, 1536], P(('groups', 'expert')), parts along dimension 0
There are 2 independent parts, one for each index of `groups`. A program takes and returns all parts, laid end to end along the dimension named above; an argument that names none is the same for every part. Nothing has to cross between parts.
Inputs may be any that keep to these rules, and one draw needn't show every extreme that they name: `route_ids`: each row names 4 different experts. In each aligned block of 32 rows no expert is named more than 32 times; one expert, the same in every block, is named exactly 32 times in every block, and the other experts' counts within a block differ by at most one.
All inputs are finite; a program needn't handle non-finite values.
Results may differ from a plain program's by a relative error of at most 0.0045.
Values may be sent and summed in bfloat16 or wider, within the bound.
A program may use at most 64 MiB of HBM per device.

v0:
```python
import functools

import jax
import jax.numpy as jnp
from jax import lax
from jax.experimental import pallas as pl
from jax.experimental.pallas import tpu as pltpu
from jax.sharding import PartitionSpec as P

MESH = pl.DeviceIdType.MESH


def gated_unit(gate_val, up_val):
    return gate_val * jax.nn.sigmoid(1.702 * gate_val) * (up_val + 1.0)


def flipped(index, bits, count):
    out = index
    power = 1
    while power < count:
        if bits // power % 2:
            out = out + power - 2 * power * lax.rem(index // power, 2)
        power *= 2
    return out


def dense_kernel(
    experts,
    tokens_ref,
    gain_ref,
    ids_ref,
    weights_ref,
    gate_ref,
    up_ref,
    down_ref,
    out_ref,
    held,
    gain,
    ids,
    weights,
    wg,
    wu,
    wd,
    xa,
    xb,
    own_out,
    x_send,
    x_recv,
    z_send,
    z_recv,
    final,
    small_sem,
    load_sem,
    swap_send,
    swap_recv,
    xa_send,
    xa_recv,
    xb_send,
    xb_recv,
    px_send,
    px_recv,
    pz_send,
    pz_recv,
    last_send,
    last_recv,
    keep_sem,
):
    me = lax.axis_index("expert")
    core = lax.axis_index("tensor")
    place = me // 2
    side = lax.rem(me, 2)
    across = {"expert": place * 2 + 1 - side}
    sibling = {"tensor": 1 - core}
    along = [{"expert": flipped(place, k, experts) * 2 + side} for k in range(experts)]
    pieces, rows, width = xa.shape[1:]
    cols = gate_ref.shape[2]
    own = pl.ds(pl.multiple_of(core * rows, rows), rows)

    barrier = pltpu.get_barrier_semaphore()
    for peer in [across, sibling] + along[1:]:
        pl.semaphore_signal(barrier, inc=1, device_id=peer, device_id_type=MESH)

    smalls = [
        pltpu.make_async_copy(src, dst, small_sem.at[i])
        for i, (src, dst) in enumerate(
            (
                (tokens_ref.at[own, :], held),
                (gain_ref, gain),
                (ids_ref, ids),
                (weights_ref, weights),
            )
        )
    ]
    for small in smalls:
        small.start()

    pairs = (
        (gate_ref.at[0], lambda half: wg.at[:, pl.ds(half * cols, cols)]),
        (up_ref.at[0], lambda half: wu.at[:, pl.ds(half * cols, cols)]),
        (down_ref.at[0], lambda half: wd.at[pl.ds(half * cols, cols), :]),
    )
    loads = [
        pltpu.make_async_copy(src, dst(0), load_sem.at[i]) for i, (src, dst) in enumerate(pairs)
    ]
    for load in loads:
        load.start()

    def part(p):
        return pl.ds(p * width, width)

    smalls[0].wait()
    resident = held[...].astype(jnp.float32)
    inv_rms = lax.rsqrt(jnp.mean(resident * resident, axis=1, keepdims=True) + 1e-05)
    smalls[1].wait()
    normed = (resident * inv_rms * gain[...].reshape(1, -1)).astype(jnp.bfloat16)
    for p in range(pieces):
        xa[0, p] = normed[:, p * width : (p + 1) * width]

    pl.semaphore_wait(barrier, experts + 1)

    def remote(src, dst, send, recv, peer):
        return pltpu.make_async_remote_copy(
            src_ref=src, dst_ref=dst, send_sem=send, recv_sem=recv, device_id=peer,
            device_id_type=MESH,
        )

    def gather_z(k, p):
        return remote(xa.at[0, p], xa.at[k, p], xa_send.at[k, p], xa_recv.at[k, p], along[k])

    def gather_x(k, p):
        return remote(xa.at[k, p], xb.at[k, p], xb_send.at[k, p], xb_recv.at[k, p], across)

    def part_x(k, p):
        return remote(
            x_send.at[k, p], x_recv.at[k, p], px_send.at[k, p], px_recv.at[k, p], across
        )

    def part_z(k, p):
        return remote(
            z_send.at[k, p], z_recv.at[k, p], pz_send.at[k, p], pz_recv.at[k, p], along[k]
        )

    swaps = [
        remote(src, dst(1), swap_send.at[i], swap_recv.at[i], sibling)
        for i, (src, dst) in enumerate(pairs)
    ]

    order = list(range(experts))
    for p in range(pieces):
        gather_x(0, p).start()
        for k in order[1:2]:
            gather_z(k, p).start()
    for k in order[2:]:
        for p in range(pieces):
            gather_z(k, p).start()
    for swap in swaps:
        swap.start()

    smalls[2].wait()
    smalls[3].wait()
    tokens_here = ids.shape[1]
    row_at = lax.broadcasted_iota(jnp.int32, (rows, tokens_here), 0) + core * rows
    on_row = row_at == lax.broadcasted_iota(jnp.int32, (rows, tokens_here), 1)
    shares = []
    for k in range(experts):
        named = jnp.where(ids[...] == flipped(place, k, experts), weights[...], 0.0)
        line = jnp.sum(named, axis=0, keepdims=True)
        shares.append(jnp.sum(jnp.where(on_row, line, 0.0), axis=1, keepdims=True))

    def forward(k):
        for p in range(pieces):
            gather_z(k, p).wait_recv()
            gather_x(k, p).start()

    def product(k, table):
        value = None
        for p in range(pieces):
            block = jnp.concatenate([xb[k, p], xa[k, p]], axis=0)
            term = jnp.dot(block, table[part(p), :], preferred_element_type=jnp.float32)
            value = term if value is None else value + term
        return value

    def compute(k):
        for p in range(pieces):
            gather_x(k, p).wait_recv()
        if k == 0:
            loads[0].wait()
            swaps[0].wait_recv()
        gate_val = product(k, wg)
        if k == 0:
            loads[1].wait()
            swaps[1].wait_recv()
        up_val = product(k, wu)
        hidden = gated_unit(gate_val, up_val).astype(jnp.bfloat16)
        if k == 0:
            loads[2].wait()
            swaps[2].wait_recv()
        for p in range(pieces):
            result = jnp.dot(hidden, wd[:, part(p)], preferred_element_type=jnp.float32)
            x_send[k, p] = result[:rows].astype(jnp.bfloat16)
            if k:
                part_x(k, p).start()
            own_out[k, p] = result[rows:]

    def close(k):
        for p in range(pieces):
            part_x(k, p).wait_recv()
            both = own_out[k, p] + x_recv[k, p].astype(jnp.float32)
            z_send[k, p] = both.astype(jnp.bfloat16)
            part_z(k, p).start()

    for step, k in enumerate(order):
        if step + 1 < experts:
            forward(order[step + 1])
        if step >= 3:
            close(order[step - 2])
        compute(k)
    for p in range(pieces):
        part_x(0, p).start()
    for k in order[max(1, experts - 2) :]:
        close(k)

    def give(p):
        there = out_ref.at[own, part(p)]
        return remote(final.at[:, part(p)], there, last_send.at[p], last_recv.at[p], sibling)

    def keep(p):
        return pltpu.make_async_copy(
            final.at[:, part(p)], out_ref.at[own, part(p)], keep_sem.at[p]
        )

    for p in range(pieces):
        part_x(0, p).wait_recv()
        both = own_out[0, p] + x_recv[0, p].astype(jnp.float32)
        own_out[0, p] = held[:, part(p)].astype(jnp.float32) + shares[0] * both
    for p in range(pieces):
        total = own_out[0, p]
        for k in order[1:]:
            part_z(k, p).wait_recv()
            total = total + shares[k] * z_recv[k, p].astype(jnp.float32)
        final[:, part(p)] = total.astype(jnp.bfloat16)
        give(p).start()
        keep(p).start()

    for p in range(pieces):
        for k in range(experts):
            gather_x(k, p).wait_send()
            part_x(k, p).wait_send()
            if k:
                gather_z(k, p).wait_send()
                part_z(k, p).wait_send()
    for swap in swaps:
        swap.wait_send()
    for p in range(pieces):
        give(p).wait()
        keep(p).wait()


def dense_layer(tokens, gain, route_ids, route_weights, w_gate, w_up, w_down):
    experts = lax.axis_size("expert") // 2
    features = tokens.shape[1]
    rows = tokens.shape[0] // lax.axis_size("tensor")
    units = 2 * w_gate.shape[2]
    pieces = 2
    hbm = pl.BlockSpec(memory_space=pl.ANY)
    half = jnp.bfloat16
    dma = pltpu.SemaphoreType.DMA
    slots = pltpu.VMEM((experts, pieces, rows, features // pieces), half)
    ids = route_ids.T
    weights = route_weights.T
    return pl.pallas_call(
        functools.partial(dense_kernel, experts),
        out_shape=jax.ShapeDtypeStruct(tokens.shape, tokens.dtype),
        in_specs=[hbm] * 7,
        out_specs=hbm,
        scratch_shapes=[
            pltpu.VMEM((rows, features), half),
            pltpu.VMEM((features,), jnp.float32),
            pltpu.VMEM(ids.shape, jnp.int32),
            pltpu.VMEM(weights.shape, jnp.float32),
            pltpu.VMEM((features, units), half),
            pltpu.VMEM((features, units), half),
            pltpu.VMEM((units, features), half),
            slots,
            slots,
            pltpu.VMEM((experts, pieces, rows, features // pieces), jnp.float32),
            slots,
            slots,
            slots,
            slots,
            pltpu.VMEM((rows, features), half),
            dma((4,)),
            dma((3,)),
            dma((3,)),
            dma((3,)),
        ]
        + [dma((experts, pieces))] * 8
        + [dma((pieces,))] * 3,
        compiler_params=pltpu.CompilerParams(
            collective_id=0, has_side_effects=True, vmem_limit_bytes=66_000_000
        ),
    )(tokens, gain, ids, weights, w_gate, w_up, w_down)


def route_tables(chosen_ids, chosen_weights, expert_count, slot_room):
    row_count, top_count = chosen_ids.shape
    matches = (chosen_ids[:, :, None] == jnp.arange(expert_count, dtype=jnp.int32)).astype(
        jnp.float32
    )
    flat_match = matches.reshape(row_count * top_count, expert_count)
    order_range = jnp.arange(row_count * top_count, dtype=jnp.int32)
    earlier = (order_range[:, None] > order_range[None, :]).astype(jnp.float32)
    before = jnp.dot(
        earlier, flat_match, precision=lax.Precision.HIGHEST, preferred_element_type=jnp.float32
    )
    position = jnp.sum(before * flat_match, axis=1).reshape(row_count, top_count).astype(jnp.int32)
    slot_index = chosen_ids * slot_room + position
    targets = jnp.arange(expert_count * slot_room, dtype=jnp.int32)
    slot_hits = slot_index[None, :, :] == targets[:, None, None]
    send_table = jnp.sum(slot_hits.astype(jnp.float32), axis=2).astype(jnp.bfloat16)
    mix_table = jnp.sum(jnp.where(slot_hits, chosen_weights[None, :, :], 0.0), axis=2)
    return (send_table, mix_table)


def routed_layer(tokens, gain, route_ids, route_weights, w_gate, w_up, w_down):
    expert_axis = lax.axis_size("expert")
    expert_count = expert_axis // 2
    tensor_count = lax.axis_size("tensor")
    own_rows = tokens.shape[0] // tensor_count
    top_count = route_ids.shape[1]
    capacity = max(2, own_rows * top_count // expert_count)
    gate_local = w_gate[0]
    up_local = w_up[0]
    down_local = w_down[0]
    first_row = lax.axis_index("tensor") * own_rows
    own_tokens = lax.dynamic_slice_in_dim(tokens, first_row, own_rows, 0)
    own_ids = lax.dynamic_slice_in_dim(route_ids, first_row, own_rows, 0)
    own_weights = lax.dynamic_slice_in_dim(route_weights, first_row, own_rows, 0)
    resident = own_tokens.astype(jnp.float32)
    inv_rms = lax.rsqrt(jnp.mean(resident * resident, axis=1, keepdims=True) + 1e-05)
    normed = (resident * inv_rms * gain).astype(jnp.bfloat16)
    send_table, mix_table = route_tables(own_ids, own_weights, expert_count, capacity)
    packed = jnp.dot(send_table, normed, preferred_element_type=jnp.float32).astype(jnp.bfloat16)
    features = packed.shape[1]
    by_expert = packed.reshape(expert_count, 1, capacity, features)
    outgoing = jnp.broadcast_to(by_expert, (expert_count, 2, capacity, features)).reshape(
        expert_axis * capacity, features
    )
    arrived = lax.all_to_all(outgoing, "expert", split_axis=0, concat_axis=0, tiled=True)
    row_piece = lax.all_gather(arrived, "tensor", axis=0, tiled=True)
    gate_val = jnp.dot(row_piece, gate_local, preferred_element_type=jnp.float32)
    up_val = jnp.dot(row_piece, up_local, preferred_element_type=jnp.float32)
    hidden = gated_unit(gate_val, up_val).astype(jnp.bfloat16)
    partial_value = lax.psum_scatter(
        jnp.dot(hidden, down_local, preferred_element_type=jnp.float32),
        "tensor",
        scatter_dimension=0,
        tiled=True,
    )
    returned = lax.all_to_all(
        partial_value.astype(jnp.bfloat16), "expert", split_axis=0, concat_axis=0, tiled=True
    ).astype(partial_value.dtype)
    expert_out = (
        returned.reshape(expert_count, 2, capacity, features)
        .sum(axis=1)
        .reshape(expert_count * capacity, features)
    )
    weighted = jnp.dot(
        mix_table.T, expert_out, precision=lax.Precision.HIGHEST, preferred_element_type=jnp.float32
    )
    finished = (resident + weighted).astype(jnp.bfloat16)
    return lax.all_gather(finished, "tensor", axis=0, tiled=True)


def per_device(tokens, gain, route_ids, route_weights, w_gate, w_up, w_down):
    experts = lax.axis_size("expert") // 2
    dense = (
        route_ids.shape[1] == experts
        and experts & (experts - 1) == 0
        and lax.axis_size("tensor") == 2
        and w_gate.shape[0] == 1
    )
    layer = dense_layer if dense else routed_layer
    return layer(tokens, gain, route_ids, route_weights, w_gate, w_up, w_down)


def solution(mesh):
    placed = (
        P(("groups", "expert"), None),
        P(),
        P(("groups", "expert"), None),
        P(("groups", "expert"), None),
        P("expert", None, "tensor"),
        P("expert", None, "tensor"),
        P("expert", "tensor", None),
    )
    return jax.shard_map(
        per_device,
        mesh=mesh,
        in_specs=placed,
        out_specs=P(("groups", "expert"), None),
        check_vma=False,
    )
```

profile of v0, /device:TPU:0, one launch (start us, length us, event | category | flops | bytes accessed | tf_op | source)
XLA Modules:
  0.0 33.5 jit_solution(485672344599027227)
XLA Ops:
  0.0 31.9 %shard_map.73 = bf16[64,1536]{1,0:T(8,128)(2,1)} custom-call(bf16[64,1536]{1,0:T(8,128)(2,1)} %tokens_ref.1, f32[1536]{0:T(1024)} %gain_ref.1, s32[4,64]{1,0:T(4,128)} %bitcast.2, f32[4,64]{1,0:T(4,128)} %bitcast.3, bf16[1,1536,384]{2,1,0:T(8,128)(2,1)} %gate_ref.1, bf16[1,1536,384]{2,1,0:T(8,128)(2,1)} %up_ref.1, bf16[1,384,1536]{2,1,0:T(8,128)(2,1)} %down_ref.1), custom_call_target="tpu_custom_call" | custom-call | tf_op jit(solution)/shard_map/pallas_call | solution.py:271
  31.9 1.6 %copy.9 = bf16[64,1536]{1,0:T(8,128)(2,1)} copy(bf16[64,1536]{1,0:T(8,128)(2,1)} %shard_map.73) | data formatting | bytes 393216
where the time goes:
time: 33.6 us; the launch traced here: 33.5 us
  Pallas kernels  31.9 us (95%)
  local copies, waits for them, and re-layouts  1.62 us (5%)
    pallas_call x1, Pallas kernels, dense_layer(): pl.pallas_call(functools.partial(dense_kernel, experts), out_shape=jax.Sh...  31.9 us
    unnamed x1, local copies, waits for them, and re-layouts  1.62 us

commit v1 on v0

v1 whole, which is shorter than its diff:
```python
import jax
import jax.numpy as jnp
from jax import lax
from jax.experimental import pallas as pl
from jax.experimental.pallas import tpu as pltpu
from jax.sharding import PartitionSpec as P

MESH = pl.DeviceIdType.MESH


def gated_unit(gate_val, up_val):
    return gate_val * jax.nn.sigmoid(1.702 * gate_val) * (up_val + 1.0)


def dense_kernel(
    tokens_ref,
    gain_ref,
    ids_ref,
    weights_ref,
    gate_ref,
    up_ref,
    down_ref,
    out_ref,
    held,
    gain,
    ids,
    weights,
    wg,
    wu,
    wd,
    own,
    slots,
    keep,
    first_out,
    first_in,
    second_out,
    second_in,
    near_out,
    near_in,
    final,
    line_out,
    line_in,
    small_sem,
    load_sem,
    swap_send,
    swap_recv,
    line_send,
    line_recv,
    spread_send,
    spread_recv,
    back_send,
    back_recv,
    near_send,
    near_recv,
    give_send,
    give_recv,
    keep_sem,
):
    me = lax.axis_index("expert")
    core = lax.axis_index("tensor")
    place = me // 2
    side = lax.rem(me, 2)
    half = place // 2
    inner = lax.rem(place + half, 2)
    is_inner = inner == 1

    def at(where, which):
        return {"expert": where * 2 + which}

    pair = place + 1 - 2 * lax.rem(place, 2)
    far_inner = 2 - half
    far_outer = 3 - 3 * half
    across = at(place, 1 - side)
    beside = at(pair, side)
    corner = at(pair, 1 - side)
    sibling = {"tensor": 1 - core}
    far_spots = (far_inner, far_outer)
    far = [at(spot, side) for spot in far_spots]
    my_far_slot = 1 - inner

    rows, features = own.shape
    cols = gate_ref.shape[2]
    batches = spread_send.shape[1]
    batch = rows // batches
    pieces, _, width = keep.shape
    scope = jax.named_scope

    barrier = pltpu.get_barrier_semaphore()

    def greet(peers):
        for peer in peers:
            pl.semaphore_signal(barrier, inc=1, device_id=peer, device_id_type=MESH)

    near_peers = [across, beside, corner, sibling]
    far_peers = [across, beside, *far, sibling]

    @pl.when(core == 0)
    def _():
        greet(near_peers)

    @pl.when(core == 1)
    def _():
        greet(far_peers)

    smalls = [
        pltpu.make_async_copy(src, dst, small_sem.at[i])
        for i, (src, dst) in enumerate(
            (
                (tokens_ref, held),
                (gain_ref, gain),
                (ids_ref, ids),
                (weights_ref, weights),
            )
        )
    ]
    for small in smalls:
        small.start()

    pairs = (
        (gate_ref.at[0], lambda part: wg.at[:, pl.ds(part * cols, cols)]),
        (up_ref.at[0], lambda part: wu.at[:, pl.ds(part * cols, cols)]),
        (down_ref.at[0], lambda part: wd.at[pl.ds(part * cols, cols), :]),
    )
    loads = [
        pltpu.make_async_copy(src, dst(0), load_sem.at[i]) for i, (src, dst) in enumerate(pairs)
    ]
    for load in loads:
        load.start()

    def remote(src, dst, send, recv, peer):
        return pltpu.make_async_remote_copy(
            src_ref=src, dst_ref=dst, send_sem=send, recv_sem=recv, device_id=peer,
            device_id_type=MESH,
        )

    swaps = [
        remote(src, dst(1), swap_send.at[i], swap_recv.at[i], sibling)
        for i, (src, dst) in enumerate(pairs)
    ]

    def rows_of(q):
        return pl.ds(q * batch, batch)

    def part(p):
        return pl.ds(p * width, width)

    with scope("w_small"):
        smalls[0].wait()
        smalls[1].wait()

    def normed(q):
        resident = held[rows_of(q), :].astype(jnp.float32)
        inv_rms = lax.rsqrt(jnp.mean(resident * resident, axis=1, keepdims=True) + 1e-05)
        return (resident * inv_rms * gain[...].reshape(1, -1)).astype(jnp.bfloat16)

    smalls[2].wait()
    smalls[3].wait()
    lanes = line_out.shape[1]
    spots = line_out.shape[0]
    spot_ids = lax.broadcasted_iota(jnp.int32, (rows, rows), 0)
    lane_ids = lax.broadcasted_iota(jnp.int32, (rows, rows), 1)

    def line_of(spot):
        named = jnp.where(ids[...] == spot, weights[...], 0.0)
        return jnp.sum(named, axis=0, keepdims=True)

    def column(line):
        return jnp.sum(jnp.where(spot_ids == lane_ids, line, 0.0), axis=1, keepdims=True)

    def ready(i):
        loads[i].wait()
        swaps[i].wait_recv()

    def hidden_of(first, fresh):
        block = slots[pl.ds(first, 2)].reshape(2 * rows, features)
        if fresh:
            with scope("w_wg"):
                ready(0)
        gate_val = jnp.dot(block, wg[...], preferred_element_type=jnp.float32)
        if fresh:
            with scope("w_wu"):
                ready(1)
        up_val = jnp.dot(block, wu[...], preferred_element_type=jnp.float32)
        value = gated_unit(gate_val, up_val).astype(jnp.bfloat16)
        if fresh:
            with scope("w_wd"):
                ready(2)
        return value

    def down(hidden, p):
        return jnp.dot(hidden, wd[:, part(p)], preferred_element_type=jnp.float32)

    def give(p):
        there = out_ref.at[:, part(p)]
        return remote(final.at[:, part(p)], there, give_send.at[p], give_recv.at[p], sibling)

    def stay(p):
        return pltpu.make_async_copy(final.at[:, part(p)], out_ref.at[:, part(p)], keep_sem.at[p])

    def hand(p):
        return remote(near_out.at[p], near_in.at[p], near_send.at[p], near_recv.at[p], sibling)

    def spread(lane, slot, q, src, peer):
        return remote(
            src.at[rows_of(q), :], slots.at[slot, rows_of(q), :], spread_send.at[lane, q],
            spread_recv.at[slot, q], peer,
        )

    lower, upper = pl.ds(0, rows), pl.ds(rows, rows)

    @pl.when(core == 0)
    def _():
        def to_across(q):
            return spread(0, 1, q, slots.at[0], across)

        def to_beside(q):
            return spread(1, 2, q, slots.at[0], beside)

        def on_to_beside(q):
            return spread(2, 3, q, slots.at[1], beside)

        def line_to(i):
            return remote(
                line_out, line_in.at[i], line_send.at[i], line_recv.at[i],
                (across, beside, corner)[i],
            )

        def back_z(p):
            return remote(
                first_out.at[p], first_in.at[p], back_send.at[0, p], back_recv.at[0, p], beside
            )

        def back_x(p):
            return remote(
                second_out.at[p, lower, :], second_in.at[p, lower, :], back_send.at[1, p],
                back_recv.at[1, p], across,
            )

        for q in range(batches):
            slots[0, rows_of(q), :] = normed(q)
        for spot in range(spots):
            line_out[spot : spot + 1, :] = line_of(spot)
        with scope("w_bar"):
            pl.semaphore_wait(barrier, len(near_peers))
        for q in range(batches):
            to_across(q).start()
            to_beside(q).start()
        for i in range(3):
            line_to(i).start()
        for swap in swaps:
            swap.start()
        for q in range(batches):
            with scope(f"w_A{q}"):
                to_across(q).wait_recv()
            on_to_beside(q).start()
        for i in range(3):
            line_to(i).wait_recv()

        def share(table):
            own_line = jnp.sum(
                jnp.where(
                    lax.broadcasted_iota(jnp.int32, (spots, lanes), 0) == place, table, 0.0
                ),
                axis=0,
                keepdims=True,
            )
            return column(own_line)

        own_share = share(line_out[...])
        shares = [share(line_in[i]) for i in range(3)]
        hidden = hidden_of(0, True)
        scales = jnp.concatenate([own_share, shares[0]], axis=0)
        for p in range(pieces):
            keep[p] = down(hidden, p) * scales
        for q in range(batches):
            with scope(f"w_P{q}"):
                to_beside(q).wait_recv()
        for q in range(batches):
            with scope(f"w_D{q}"):
                on_to_beside(q).wait_recv()
        hidden = hidden_of(2, False)
        scales = jnp.concatenate([shares[1], shares[2]], axis=0)
        for p in range(pieces):
            first_out[p] = (down(hidden, p) * scales).astype(jnp.bfloat16)
            back_z(p).start()
        for p in range(pieces):
            with scope(f"w_bz{p}"):
                back_z(p).wait_recv()
            both = keep[p] + first_in[p].astype(jnp.float32)
            second_out[p, lower, :] = both[rows:].astype(jnp.bfloat16)
            back_x(p).start()
            keep[p, lower, :] = both[:rows] + held[:, part(p)].astype(jnp.float32)
        for p in range(pieces):
            with scope(f"w_bx{p}"):
                back_x(p).wait_recv()
            near_out[p] = keep[p, lower, :] + second_in[p, lower, :].astype(jnp.float32)
            hand(p).start()
        for q in range(batches):
            to_across(q).wait_send()
            to_beside(q).wait_send()
            on_to_beside(q).wait_send()
        for i in range(3):
            line_to(i).wait_send()
        for p in range(pieces):
            back_z(p).wait_send()
            back_x(p).wait_send()
            hand(p).wait_send()
        for swap in swaps:
            swap.wait_send()
        with scope("w_give"):
            for p in range(pieces):
                give(p).wait_recv()

    @pl.when(core == 1)
    def _():
        def outward(q):
            return remote(
                own.at[rows_of(q), :], slots.at[my_far_slot, rows_of(q), :], spread_send.at[0, q],
                spread_recv.at[my_far_slot, q], far[0],
            )

        def arrived(s, q):
            return spread(1 + s, s, q, slots.at[s], beside)

        def sideways(s, q):
            return spread(3 + s, 2 + s, q, slots.at[s], across)

        def back_x(p):
            return remote(
                first_out.at[p], first_in.at[p], back_send.at[0, p], back_recv.at[0, p], across
            )

        def back_z(s, p):
            return remote(
                second_out.at[p, (lower, upper)[s], :],
                second_in.at[p, pl.ds(pl.multiple_of(my_far_slot * rows, rows), rows), :],
                back_send.at[1 + s, p],
                back_recv.at[1 + my_far_slot, p],
                far[s],
            )

        def came_z(s, p):
            return remote(
                second_out.at[p, (lower, upper)[s], :], second_in.at[p, (lower, upper)[s], :],
                back_send.at[1 + s, p], back_recv.at[1 + s, p], far[s],
            )

        for q in range(batches):
            own[rows_of(q), :] = normed(q)
        with scope("w_bar"):
            pl.semaphore_wait(barrier, len(far_peers))
        for q in range(batches):
            outward(q).start()
        for swap in swaps:
            swap.start()
        shares = [column(line_of(spot)) for spot in far_spots]
        for q in range(batches):
            for s in range(2):
                with scope(f"w_F{s}{q}"):
                    arrived(s, q).wait_recv()

                @pl.when(is_inner)
                def _():
                    arrived(s, q).start()

                sideways(s, q).start()
        hidden = hidden_of(0, True)
        for p in range(pieces):
            keep[p] = down(hidden, p)
        for q in range(batches):
            for s in range(2):
                with scope(f"w_G{s}{q}"):
                    sideways(s, q).wait_recv()
        hidden = hidden_of(2, False)
        for p in range(pieces):
            first_out[p] = down(hidden, p).astype(jnp.bfloat16)
            back_x(p).start()
        for p in range(pieces):
            with scope(f"w_bx{p}"):
                back_x(p).wait_recv()
            second_out[p] = (keep[p] + first_in[p].astype(jnp.float32)).astype(jnp.bfloat16)
            for s in range(2):
                back_z(s, p).start()
        for p in range(pieces):
            with scope(f"w_near{p}"):
                hand(p).wait_recv()
            total = near_in[p]
            for s in range(2):
                with scope(f"w_bz{s}{p}"):
                    came_z(s, p).wait_recv()
                total = total + shares[s] * second_in[p, (lower, upper)[s], :].astype(jnp.float32)
            final[:, part(p)] = total.astype(jnp.bfloat16)
            give(p).start()
            stay(p).start()
        for q in range(batches):
            outward(q).wait_send()
            for s in range(2):
                sideways(s, q).wait_send()

                @pl.when(is_inner)
                def _():
                    arrived(s, q).wait_send()

        for p in range(pieces):
            back_x(p).wait_send()
            for s in range(2):
                back_z(s, p).wait_send()
        for swap in swaps:
            swap.wait_send()
        with scope("w_end"):
            for p in range(pieces):
                give(p).wait_send()
                stay(p).wait()


def dense_layer(tokens, gain, route_ids, route_weights, w_gate, w_up, w_down):
    rows, features = tokens.shape
    units = 2 * w_gate.shape[2]
    batches = rows // 16
    pieces = 3
    width = features // pieces
    hbm = pl.BlockSpec(memory_space=pl.ANY)
    half = jnp.bfloat16
    dma = pltpu.SemaphoreType.DMA
    ids = route_ids.T
    weights = route_weights.T
    travel = pltpu.VMEM((pieces, 2 * rows, width), half)
    return pl.pallas_call(
        dense_kernel,
        out_shape=jax.ShapeDtypeStruct(tokens.shape, tokens.dtype),
        in_specs=[hbm] * 7,
        out_specs=hbm,
        scratch_shapes=[
            pltpu.VMEM((rows, features), half),
            pltpu.VMEM((features,), jnp.float32),
            pltpu.VMEM(ids.shape, jnp.int32),
            pltpu.VMEM(weights.shape, jnp.float32),
            pltpu.VMEM((features, units), half),
            pltpu.VMEM((features, units), half),
            pltpu.VMEM((units, features), half),
            pltpu.VMEM((rows, features), half),
            pltpu.VMEM((4, rows, features), half),
            pltpu.VMEM((pieces, 2 * rows, width), jnp.float32),
            travel,
            travel,
            travel,
            travel,
            pltpu.VMEM((pieces, rows, width), jnp.float32),
            pltpu.VMEM((pieces, rows, width), jnp.float32),
            pltpu.VMEM((rows, features), half),
            pltpu.VMEM(weights.shape, jnp.float32),
            pltpu.VMEM((3, *weights.shape), jnp.float32),
            dma((4,)),
            dma((3,)),
            dma((3,)),
            dma((3,)),
            dma((3,)),
            dma((3,)),
            dma((5, batches)),
            dma((4, batches)),
            dma((3, pieces)),
            dma((3, pieces)),
        ]
        + [dma((pieces,))] * 5,
        compiler_params=pltpu.CompilerParams(
            collective_id=0, has_side_effects=True, vmem_limit_bytes=66_000_000
        ),
    )(tokens, gain, ids, weights, w_gate, w_up, w_down)


def route_tables(chosen_ids, chosen_weights, expert_count, slot_room):
    row_count, top_count = chosen_ids.shape
    matches = (chosen_ids[:, :, None] == jnp.arange(expert_count, dtype=jnp.int32)).astype(
        jnp.float32
    )
    flat_match = matches.reshape(row_count * top_count, expert_count)
    order_range = jnp.arange(row_count * top_count, dtype=jnp.int32)
    earlier = (order_range[:, None] > order_range[None, :]).astype(jnp.float32)
    before = jnp.dot(
        earlier, flat_match, precision=lax.Precision.HIGHEST, preferred_element_type=jnp.float32
    )
    position = jnp.sum(before * flat_match, axis=1).reshape(row_count, top_count).astype(jnp.int32)
    slot_index = chosen_ids * slot_room + position
    targets = jnp.arange(expert_count * slot_room, dtype=jnp.int32)
    slot_hits = slot_index[None, :, :] == targets[:, None, None]
    send_table = jnp.sum(slot_hits.astype(jnp.float32), axis=2).astype(jnp.bfloat16)
    mix_table = jnp.sum(jnp.where(slot_hits, chosen_weights[None, :, :], 0.0), axis=2)
    return (send_table, mix_table)


def routed_layer(tokens, gain, route_ids, route_weights, w_gate, w_up, w_down):
    expert_axis = lax.axis_size("expert")
    expert_count = expert_axis // 2
    tensor_count = lax.axis_size("tensor")
    own_rows = tokens.shape[0] // tensor_count
    top_count = route_ids.shape[1]
    capacity = max(2, own_rows * top_count // expert_count)
    gate_local = w_gate[0]
    up_local = w_up[0]
    down_local = w_down[0]
    first_row = lax.axis_index("tensor") * own_rows
    own_tokens = lax.dynamic_slice_in_dim(tokens, first_row, own_rows, 0)
    own_ids = lax.dynamic_slice_in_dim(route_ids, first_row, own_rows, 0)
    own_weights = lax.dynamic_slice_in_dim(route_weights, first_row, own_rows, 0)
    resident = own_tokens.astype(jnp.float32)
    inv_rms = lax.rsqrt(jnp.mean(resident * resident, axis=1, keepdims=True) + 1e-05)
    normed = (resident * inv_rms * gain).astype(jnp.bfloat16)
    send_table, mix_table = route_tables(own_ids, own_weights, expert_count, capacity)
    packed = jnp.dot(send_table, normed, preferred_element_type=jnp.float32).astype(jnp.bfloat16)
    features = packed.shape[1]
    by_expert = packed.reshape(expert_count, 1, capacity, features)
    outgoing = jnp.broadcast_to(by_expert, (expert_count, 2, capacity, features)).reshape(
        expert_axis * capacity, features
    )
    arrived = lax.all_to_all(outgoing, "expert", split_axis=0, concat_axis=0, tiled=True)
    row_piece = lax.all_gather(arrived, "tensor", axis=0, tiled=True)
    gate_val = jnp.dot(row_piece, gate_local, preferred_element_type=jnp.float32)
    up_val = jnp.dot(row_piece, up_local, preferred_element_type=jnp.float32)
    hidden = gated_unit(gate_val, up_val).astype(jnp.bfloat16)
    partial_value = lax.psum_scatter(
        jnp.dot(hidden, down_local, preferred_element_type=jnp.float32),
        "tensor",
        scatter_dimension=0,
        tiled=True,
    )
    returned = lax.all_to_all(
        partial_value.astype(jnp.bfloat16), "expert", split_axis=0, concat_axis=0, tiled=True
    ).astype(partial_value.dtype)
    expert_out = (
        returned.reshape(expert_count, 2, capacity, features)
        .sum(axis=1)
        .reshape(expert_count * capacity, features)
    )
    weighted = jnp.dot(
        mix_table.T, expert_out, precision=lax.Precision.HIGHEST, preferred_element_type=jnp.float32
    )
    finished = (resident + weighted).astype(jnp.bfloat16)
    return lax.all_gather(finished, "tensor", axis=0, tiled=True)


def per_device(tokens, gain, route_ids, route_weights, w_gate, w_up, w_down):
    experts = lax.axis_size("expert") // 2
    dense = (
        route_ids.shape[1] == experts
        and experts == 4
        and lax.axis_size("tensor") == 2
        and w_gate.shape[0] == 1
    )
    layer = dense_layer if dense else routed_layer
    return layer(tokens, gain, route_ids, route_weights, w_gate, w_up, w_down)


def solution(mesh):
    placed = (
        P(("groups", "expert"), None),
        P(),
        P(("groups", "expert"), None),
        P(("groups", "expert"), None),
        P("expert", None, "tensor"),
        P("expert", None, "tensor"),
        P("expert", "tensor", None),
    )
    return jax.shard_map(
        per_device,
        mesh=mesh,
        in_specs=placed,
        out_specs=P(("groups", "expert"), None),
        check_vma=False,
    )
```

time: 33.6 us -> 34.7 us (1.033)
  Pallas kernels: 31.9 us -> 33 us
    pallas_call x1, Pallas kernels: 31.9 us -> 33 us  [dense_layer(): pl.pallas_call(dense_kernel, out_shape=jax.ShapeDtypeStruct(tokens.shape,...]
where the time goes in v1:
time: 34.7 us; the launch traced here: 34.6 us
  Pallas kernels  33 us (95%)
  local copies, waits for them, and re-layouts  1.62 us (5%)
    pallas_call x1, Pallas kernels, dense_layer(): pl.pallas_call(dense_kernel, out_shape=jax.ShapeDtypeStruct(tokens.shape,...  33 us
    unnamed x1, local copies, waits for them, and re-layouts  1.62 us

profile of v1, /device:TPU:0, one launch (start us, length us, event | category | flops | bytes accessed | tf_op | source)
XLA Modules:
  0.0 34.6 jit_solution(16831875702697436851)
XLA Ops:
  0.0 33.0 %shard_map.73 = bf16[64,1536]{1,0:T(8,128)(2,1)} custom-call(bf16[64,1536]{1,0:T(8,128)(2,1)} %tokens_ref.1, f32[1536]{0:T(1024)} %gain_ref.1, s32[4,64]{1,0:T(4,128)} %bitcast.2, f32[4,64]{1,0:T(4,128)} %bitcast.3, bf16[1,1536,384]{2,1,0:T(8,128)(2,1)} %gate_ref.1, bf16[1,1536,384]{2,1,0:T(8,128)(2,1)} %up_ref.1, bf16[1,384,1536]{2,1,0:T(8,128)(2,1)} %down_ref.1), custom_call_target="tpu_custom_call" | custom-call | tf_op jit(solution)/shard_map/pallas_call | solution.py:428
  33.0 1.6 %copy.9 = bf16[64,1536]{1,0:T(8,128)(2,1)} copy(bf16[64,1536]{1,0:T(8,128)(2,1)} %shard_map.73) | data formatting | bytes 393216

commit v2 on v1

--- a/solution.py
+++ b/solution.py
@@ -35,8 +35,13 @@
     first_in,
     second_out,
     second_in,
-    near_out,
-    near_in,
+    own_pair,
+    other_pair,
+    from_beside,
+    from_across,
+    from_corner,
+    to_cross,
+    to_merge,
     final,
     line_out,
     line_in,
@@ -51,6 +56,7 @@
     back_send,
     back_recv,
     near_send,
+    pair_recv,
     near_recv,
     give_send,
     give_recv,
@@ -63,6 +69,7 @@
     half = place // 2
     inner = lax.rem(place + half, 2)
     is_inner = inner == 1
+    is_outer = inner == 0
 
     def at(where, which):
         return {"expert": where * 2 + which}
@@ -80,7 +87,7 @@
 
     rows, features = own.shape
     cols = gate_ref.shape[2]
-    batches = spread_send.shape[1]
+    batches = spread_recv.shape[1]
     batch = rows // batches
     pieces, _, width = keep.shape
     scope = jax.named_scope
@@ -91,6 +98,9 @@
         for peer in peers:
             pl.semaphore_signal(barrier, inc=1, device_id=peer, device_id_type=MESH)
 
+    def on(peer, which):
+        return {**peer, "tensor": which}
+
     near_peers = [across, beside, corner, sibling]
     far_peers = [across, beside, *far, sibling]
 
@@ -100,7 +110,7 @@
 
     @pl.when(core == 1)
     def _():
-        greet(far_peers)
+        greet([*far_peers, on(across, 0), on(beside, 0)])
 
     smalls = [
         pltpu.make_async_copy(src, dst, small_sem.at[i])
@@ -192,21 +202,33 @@
 
     def give(p):
         there = out_ref.at[:, part(p)]
-        return remote(final.at[:, part(p)], there, give_send.at[p], give_recv.at[p], sibling)
+        return remote(final.at[:, part(p)], there, give_send, give_recv, sibling)
 
     def stay(p):
-        return pltpu.make_async_copy(final.at[:, part(p)], out_ref.at[:, part(p)], keep_sem.at[p])
-
-    def hand(p):
-        return remote(near_out.at[p], near_in.at[p], near_send.at[p], near_recv.at[p], sibling)
+        return pltpu.make_async_copy(final.at[:, part(p)], out_ref.at[:, part(p)], keep_sem)
+
+    def whole(ref, sem):
+        return pltpu.make_async_copy(ref, ref, sem)
 
     def spread(lane, slot, q, src, peer):
         return remote(
-            src.at[rows_of(q), :], slots.at[slot, rows_of(q), :], spread_send.at[lane, q],
+            src.at[rows_of(q), :], slots.at[slot, rows_of(q), :], spread_send.at[lane],
             spread_recv.at[slot, q], peer,
         )
 
     lower, upper = pl.ds(0, rows), pl.ds(rows, rows)
+    both_halves = pl.ds(0, 2 * rows)
+
+    def cross(p, src):
+        return remote(
+            src, from_across.at[p], near_send.at[2], near_recv.at[1, p], on(across, 1)
+        )
+
+    def along(p, src, rows_there):
+        return remote(
+            src, from_beside.at[p, rows_there, :], near_send.at[1], near_recv.at[0, p],
+            on(beside, 1),
+        )
 
     @pl.when(core == 0)
     def _():
@@ -218,6 +240,9 @@
 
         def on_to_beside(q):
             return spread(2, 3, q, slots.at[1], beside)
+
+        def on_to_across(q):
+            return spread(3, 3, q, slots.at[2], across)
 
         def line_to(i):
             return remote(
@@ -225,23 +250,12 @@
                 (across, beside, corner)[i],
             )
 
-        def back_z(p):
-            return remote(
-                first_out.at[p], first_in.at[p], back_send.at[0, p], back_recv.at[0, p], beside
-            )
-
-        def back_x(p):
-            return remote(
-                second_out.at[p, lower, :], second_in.at[p, lower, :], back_send.at[1, p],
-                back_recv.at[1, p], across,
-            )
-
         for q in range(batches):
             slots[0, rows_of(q), :] = normed(q)
         for spot in range(spots):
             line_out[spot : spot + 1, :] = line_of(spot)
         with scope("w_bar"):
-            pl.semaphore_wait(barrier, len(near_peers))
+            pl.semaphore_wait(barrier, len(near_peers) + 2)
         for q in range(batches):
             to_across(q).start()
             to_beside(q).start()
@@ -252,7 +266,14 @@
         for q in range(batches):
             with scope(f"w_A{q}"):
                 to_across(q).wait_recv()
-            on_to_beside(q).start()
+
+            @pl.when(is_outer)
+            def _():
+                on_to_beside(q).start()
+                with scope(f"w_Po{q}"):
+                    to_beside(q).wait_recv()
+                on_to_across(q).start()
+
         for i in range(3):
             line_to(i).wait_recv()
 
@@ -271,51 +292,70 @@
         hidden = hidden_of(0, True)
         scales = jnp.concatenate([own_share, shares[0]], axis=0)
         for p in range(pieces):
-            keep[p] = down(hidden, p) * scales
-        for q in range(batches):
-            with scope(f"w_P{q}"):
-                to_beside(q).wait_recv()
+            first_out[p] = (down(hidden, p) * scales).astype(jnp.bfloat16)
+
+        def hand_pair(src, dst, i):
+            return remote(src, dst, near_send.at[3 * i], pair_recv.at[i], sibling)
+
+        @pl.when(is_inner)
+        def _():
+            for p in range(pieces):
+                hand_pair(first_out.at[p], own_pair.at[p], 0).start()
+            for q in range(batches):
+                with scope(f"w_P{q}"):
+                    to_beside(q).wait_recv()
+
+        @pl.when(is_outer)
+        def _():
+            for p in range(pieces):
+                hand_pair(first_out.at[p, lower, :], own_pair.at[p, lower, :], 0).start()
+
         for q in range(batches):
             with scope(f"w_D{q}"):
                 on_to_beside(q).wait_recv()
         hidden = hidden_of(2, False)
         scales = jnp.concatenate([shares[1], shares[2]], axis=0)
         for p in range(pieces):
-            first_out[p] = (down(hidden, p) * scales).astype(jnp.bfloat16)
-            back_z(p).start()
-        for p in range(pieces):
-            with scope(f"w_bz{p}"):
-                back_z(p).wait_recv()
-            both = keep[p] + first_in[p].astype(jnp.float32)
-            second_out[p, lower, :] = both[rows:].astype(jnp.bfloat16)
-            back_x(p).start()
-            keep[p, lower, :] = both[:rows] + held[:, part(p)].astype(jnp.float32)
-        for p in range(pieces):
-            with scope(f"w_bx{p}"):
-                back_x(p).wait_recv()
-            near_out[p] = keep[p, lower, :] + second_in[p, lower, :].astype(jnp.float32)
-            hand(p).start()
-        for q in range(batches):
-            to_across(q).wait_send()
-            to_beside(q).wait_send()
-            on_to_beside(q).wait_send()
+            second_out[p] = (down(hidden, p) * scales).astype(jnp.bfloat16)
+
+            @pl.when(is_inner)
+            def _():
+                hand_pair(second_out.at[p], other_pair.at[p], 1).start()
+
+            @pl.when(is_outer)
+            def _():
+                along(p, second_out.at[p], both_halves).start()
+
+        whole(slots.at[0], spread_send.at[0]).wait()
+        whole(slots.at[0], spread_send.at[1]).wait()
         for i in range(3):
             line_to(i).wait_send()
-        for p in range(pieces):
-            back_z(p).wait_send()
-            back_x(p).wait_send()
-            hand(p).wait_send()
+
+        @pl.when(is_outer)
+        def _():
+            for p in range(pieces):
+                cross(p, first_out.at[p, upper, :]).start()
+            whole(slots.at[1], spread_send.at[2]).wait()
+            whole(slots.at[2], spread_send.at[3]).wait()
+            whole(first_out.at[:, lower, :], near_send.at[0]).wait()
+            whole(second_out, near_send.at[1]).wait()
+            whole(first_out.at[:, upper, :], near_send.at[2]).wait()
+
+        @pl.when(is_inner)
+        def _():
+            whole(first_out, near_send.at[0]).wait()
+            whole(second_out, near_send.at[3]).wait()
+
         for swap in swaps:
             swap.wait_send()
         with scope("w_give"):
-            for p in range(pieces):
-                give(p).wait_recv()
+            whole(final, give_recv).wait()
 
     @pl.when(core == 1)
     def _():
         def outward(q):
             return remote(
-                own.at[rows_of(q), :], slots.at[my_far_slot, rows_of(q), :], spread_send.at[0, q],
+                own.at[rows_of(q), :], slots.at[my_far_slot, rows_of(q), :], spread_send.at[0],
                 spread_recv.at[my_far_slot, q], far[0],
             )
 
@@ -327,22 +367,25 @@
 
         def back_x(p):
             return remote(
-                first_out.at[p], first_in.at[p], back_send.at[0, p], back_recv.at[0, p], across
+                first_out.at[p], first_in.at[p], back_send.at[0], back_recv.at[0, p], across
             )
 
         def back_z(s, p):
             return remote(
                 second_out.at[p, (lower, upper)[s], :],
                 second_in.at[p, pl.ds(pl.multiple_of(my_far_slot * rows, rows), rows), :],
-                back_send.at[1 + s, p],
+                back_send.at[1],
                 back_recv.at[1 + my_far_slot, p],
                 far[s],
             )
 
         def came_z(s, p):
+            return whole(second_in.at[p, (lower, upper)[s], :], back_recv.at[1 + s, p])
+
+        def cross_corner(p):
             return remote(
-                second_out.at[p, (lower, upper)[s], :], second_in.at[p, (lower, upper)[s], :],
-                back_send.at[1 + s, p], back_recv.at[1 + s, p], far[s],
+                other_pair.at[p, upper, :], from_corner.at[p], near_send.at[0],
+                near_recv.at[2, p], across,
             )
 
         for q in range(batches):
@@ -375,49 +418,91 @@
         for p in range(pieces):
             first_out[p] = down(hidden, p).astype(jnp.bfloat16)
             back_x(p).start()
+
+        @pl.when(is_inner)
+        def _():
+            with scope("w_i2"):
+                whole(other_pair, pair_recv.at[1]).wait()
+            for p in range(pieces):
+                cross_corner(p).start()
+
         for p in range(pieces):
             with scope(f"w_bx{p}"):
                 back_x(p).wait_recv()
             second_out[p] = (keep[p] + first_in[p].astype(jnp.float32)).astype(jnp.bfloat16)
             for s in range(2):
                 back_z(s, p).start()
+
+        @pl.when(is_inner)
+        def _():
+            with scope("w_i1"):
+                whole(own_pair, pair_recv.at[0]).wait()
+            for p in range(pieces):
+                with scope(f"w_iz{p}"):
+                    whole(from_beside.at[p], near_recv.at[0, p]).wait()
+                sums = own_pair[p, upper, :].astype(jnp.float32)
+                sums = sums + from_beside[p, upper, :].astype(jnp.float32)
+                to_cross[p] = sums.astype(jnp.bfloat16)
+                cross(p, to_cross.at[p]).start()
+            for p in range(pieces):
+                with scope(f"w_ic{p}"):
+                    cross_corner(p).wait_recv()
+                sums = other_pair[p, lower, :].astype(jnp.float32)
+                sums = sums + from_corner[p].astype(jnp.float32)
+                to_merge[p] = sums.astype(jnp.bfloat16)
+                along(p, to_merge.at[p], lower).start()
+
+        @pl.when(is_outer)
+        def _():
+            with scope("w_o1"):
+                whole(own_pair.at[:, lower, :], pair_recv.at[0]).wait()
+
         for p in range(pieces):
-            with scope(f"w_near{p}"):
-                hand(p).wait_recv()
-            total = near_in[p]
+            with scope(f"w_xA{p}"):
+                whole(from_across.at[p], near_recv.at[1, p]).wait()
+
+            @pl.when(is_outer)
+            def _():
+                with scope(f"w_oz{p}"):
+                    whole(from_beside.at[p, lower, :], near_recv.at[0, p]).wait()
+
+            total = held[:, part(p)].astype(jnp.float32)
+            total = total + own_pair[p, lower, :].astype(jnp.float32)
+            total = total + from_beside[p, lower, :].astype(jnp.float32)
+            total = total + from_across[p].astype(jnp.float32)
             for s in range(2):
                 with scope(f"w_bz{s}{p}"):
-                    came_z(s, p).wait_recv()
+                    came_z(s, p).wait()
                 total = total + shares[s] * second_in[p, (lower, upper)[s], :].astype(jnp.float32)
             final[:, part(p)] = total.astype(jnp.bfloat16)
             give(p).start()
             stay(p).start()
-        for q in range(batches):
-            outward(q).wait_send()
+        whole(own, spread_send.at[0]).wait()
+        for s in range(2):
+            whole(slots.at[s], spread_send.at[3 + s]).wait()
+        whole(first_out, back_send.at[0]).wait()
+        whole(second_out, back_send.at[1]).wait()
+
+        @pl.when(is_inner)
+        def _():
             for s in range(2):
-                sideways(s, q).wait_send()
-
-                @pl.when(is_inner)
-                def _():
-                    arrived(s, q).wait_send()
-
-        for p in range(pieces):
-            back_x(p).wait_send()
-            for s in range(2):
-                back_z(s, p).wait_send()
+                whole(slots.at[s], spread_send.at[1 + s]).wait()
+            whole(from_corner, near_send.at[0]).wait()
+            whole(to_merge, near_send.at[1]).wait()
+            whole(to_cross, near_send.at[2]).wait()
+
         for swap in swaps:
             swap.wait_send()
         with scope("w_end"):
-            for p in range(pieces):
-                give(p).wait_send()
-                stay(p).wait()
+            whole(final, give_send).wait()
+            whole(final, keep_sem).wait()
 
 
 def dense_layer(tokens, gain, route_ids, route_weights, w_gate, w_up, w_down):
     rows, features = tokens.shape
     units = 2 * w_gate.shape[2]
     batches = rows // 16
-    pieces = 3
+    pieces = 6
     width = features // pieces
     hbm = pl.BlockSpec(memory_space=pl.ANY)
     half = jnp.bfloat16
@@ -425,6 +510,7 @@
     ids = route_ids.T
     weights = route_weights.T
     travel = pltpu.VMEM((pieces, 2 * rows, width), half)
+    single = pltpu.VMEM((pieces, rows, width), half)
     return pl.pallas_call(
         dense_kernel,
         out_shape=jax.ShapeDtypeStruct(tokens.shape, tokens.dtype),
@@ -441,12 +527,10 @@
             pltpu.VMEM((rows, features), half),
             pltpu.VMEM((4, rows, features), half),
             pltpu.VMEM((pieces, 2 * rows, width), jnp.float32),
-            travel,
-            travel,
-            travel,
-            travel,
-            pltpu.VMEM((pieces, rows, width), jnp.float32),
-            pltpu.VMEM((pieces, rows, width), jnp.float32),
+        ]
+        + [travel] * 7
+        + [single] * 4
+        + [
             pltpu.VMEM((rows, features), half),
             pltpu.VMEM(weights.shape, jnp.float32),
             pltpu.VMEM((3, *weights.shape), jnp.float32),
@@ -456,12 +540,17 @@
             dma((3,)),
             dma((3,)),
             dma((3,)),
-            dma((5, batches)),
+            dma((5,)),
             dma((4, batches)),
+            dma((2,)),
             dma((3, pieces)),
+            dma((4,)),
+            dma((2,)),
             dma((3, pieces)),
-        ]
-        + [dma((pieces,))] * 5,
+            dma,
+            dma,
+            dma,
+        ],
         compiler_params=pltpu.CompilerParams(
             collective_id=0, has_side_effects=True, vmem_limit_bytes=66_000_000
         ),

time: 34.7 us -> 32.1 us (0.925)
  Pallas kernels: 33 us -> 30.4 us
    pallas_call x1, Pallas kernels: 33 us -> 30.4 us  [dense_layer(): pl.pallas_call(dense_kernel, out_shape=jax.ShapeDtypeStruct(tokens.shape,...]
where the time goes in v2:
time: 32.1 us; the launch traced here: 32 us
  Pallas kernels  30.4 us (95%)
  local copies, waits for them, and re-layouts  1.62 us (5%)
    pallas_call x1, Pallas kernels, dense_layer(): pl.pallas_call(dense_kernel, out_shape=jax.ShapeDtypeStruct(tokens.shape,...  30.4 us
    unnamed x1, local copies, waits for them, and re-layouts  1.62 us

profile of v2, /device:TPU:0, one launch (start us, length us, event | category | flops | bytes accessed | tf_op | source)
XLA Modules:
  0.0 32.0 jit_solution(11341654680956946807)
XLA Ops:
  0.0 30.4 %shard_map.73 = bf16[64,1536]{1,0:T(8,128)(2,1)} custom-call(bf16[64,1536]{1,0:T(8,128)(2,1)} %tokens_ref.1, f32[1536]{0:T(1024)} %gain_ref.1, s32[4,64]{1,0:T(4,128)} %bitcast.2, f32[4,64]{1,0:T(4,128)} %bitcast.3, bf16[1,1536,384]{2,1,0:T(8,128)(2,1)} %gate_ref.1, bf16[1,1536,384]{2,1,0:T(8,128)(2,1)} %up_ref.1, bf16[1,384,1536]{2,1,0:T(8,128)(2,1)} %down_ref.1), custom_call_target="tpu_custom_call" | custom-call | tf_op jit(solution)/shard_map/pallas_call | solution.py:514
  30.4 1.6 %copy.9 = bf16[64,1536]{1,0:T(8,128)(2,1)} copy(bf16[64,1536]{1,0:T(8,128)(2,1)} %shard_map.73) | data formatting | bytes 393216

commit v3 on v2

--- a/solution.py
+++ b/solution.py
@@ -42,7 +42,6 @@
     from_corner,
     to_cross,
     to_merge,
-    final,
     line_out,
     line_in,
     small_sem,
@@ -53,6 +52,7 @@
     line_recv,
     spread_send,
     spread_recv,
+    rest_recv,
     back_send,
     back_recv,
     near_send,
@@ -60,7 +60,6 @@
     near_recv,
     give_send,
     give_recv,
-    keep_sem,
 ):
     me = lax.axis_index("expert")
     core = lax.axis_index("tensor")
@@ -88,6 +87,7 @@
     rows, features = own.shape
     cols = gate_ref.shape[2]
     batches = spread_recv.shape[1]
+    groups = near_recv.shape[1]
     batch = rows // batches
     pieces, _, width = keep.shape
     scope = jax.named_scope
@@ -202,47 +202,50 @@
 
     def give(p):
         there = out_ref.at[:, part(p)]
-        return remote(final.at[:, part(p)], there, give_send, give_recv, sibling)
-
-    def stay(p):
-        return pltpu.make_async_copy(final.at[:, part(p)], out_ref.at[:, part(p)], keep_sem)
+        return remote(there, there, give_send, give_recv, sibling)
 
     def whole(ref, sem):
         return pltpu.make_async_copy(ref, ref, sem)
 
-    def spread(lane, slot, q, src, peer):
+    def spread(lane, slot, q, src, peer, recv):
         return remote(
-            src.at[rows_of(q), :], slots.at[slot, rows_of(q), :], spread_send.at[lane],
-            spread_recv.at[slot, q], peer,
+            src.at[rows_of(q), :], slots.at[slot, rows_of(q), :], spread_send.at[lane], recv, peer
         )
+
+    def group(p):
+        return p * groups // pieces
+
+    def grouped(ref, i, g):
+        span = pieces // groups
+        return whole(ref.at[pl.ds(g * span, span)], near_recv.at[i, g])
 
     lower, upper = pl.ds(0, rows), pl.ds(rows, rows)
     both_halves = pl.ds(0, 2 * rows)
 
     def cross(p, src):
         return remote(
-            src, from_across.at[p], near_send.at[2], near_recv.at[1, p], on(across, 1)
+            src, from_across.at[p], near_send.at[2], near_recv.at[1, group(p)], on(across, 1)
         )
 
     def along(p, src, rows_there):
         return remote(
-            src, from_beside.at[p, rows_there, :], near_send.at[1], near_recv.at[0, p],
+            src, from_beside.at[p, rows_there, :], near_send.at[1], near_recv.at[0, group(p)],
             on(beside, 1),
         )
 
     @pl.when(core == 0)
     def _():
         def to_across(q):
-            return spread(0, 1, q, slots.at[0], across)
+            return spread(0, 1, q, slots.at[0], across, spread_recv.at[0, q])
 
         def to_beside(q):
-            return spread(1, 2, q, slots.at[0], beside)
+            return spread(1, 2, q, slots.at[0], beside, spread_recv.at[1, q])
 
         def on_to_beside(q):
-            return spread(2, 3, q, slots.at[1], beside)
+            return spread(2, 3, q, slots.at[1], beside, rest_recv.at[0])
 
         def on_to_across(q):
-            return spread(3, 3, q, slots.at[2], across)
+            return spread(3, 3, q, slots.at[2], across, rest_recv.at[0])
 
         def line_to(i):
             return remote(
@@ -256,11 +259,11 @@
             line_out[spot : spot + 1, :] = line_of(spot)
         with scope("w_bar"):
             pl.semaphore_wait(barrier, len(near_peers) + 2)
+        for i in range(3):
+            line_to(i).start()
         for q in range(batches):
             to_across(q).start()
             to_beside(q).start()
-        for i in range(3):
-            line_to(i).start()
         for swap in swaps:
             swap.start()
         for q in range(batches):
@@ -273,9 +276,6 @@
                 with scope(f"w_Po{q}"):
                     to_beside(q).wait_recv()
                 on_to_across(q).start()
-
-        for i in range(3):
-            line_to(i).wait_recv()
 
         def share(table):
             own_line = jnp.sum(
@@ -287,9 +287,12 @@
             )
             return column(own_line)
 
+        hidden = hidden_of(0, True)
+        with scope("w_line"):
+            for i in range(3):
+                line_to(i).wait_recv()
         own_share = share(line_out[...])
         shares = [share(line_in[i]) for i in range(3)]
-        hidden = hidden_of(0, True)
         scales = jnp.concatenate([own_share, shares[0]], axis=0)
         for p in range(pieces):
             first_out[p] = (down(hidden, p) * scales).astype(jnp.bfloat16)
@@ -310,9 +313,8 @@
             for p in range(pieces):
                 hand_pair(first_out.at[p, lower, :], own_pair.at[p, lower, :], 0).start()
 
-        for q in range(batches):
-            with scope(f"w_D{q}"):
-                on_to_beside(q).wait_recv()
+        with scope("w_D"):
+            whole(slots.at[3], rest_recv.at[0]).wait()
         hidden = hidden_of(2, False)
         scales = jnp.concatenate([shares[1], shares[2]], axis=0)
         for p in range(pieces):
@@ -349,7 +351,7 @@
         for swap in swaps:
             swap.wait_send()
         with scope("w_give"):
-            whole(final, give_recv).wait()
+            whole(out_ref, give_recv).wait()
 
     @pl.when(core == 1)
     def _():
@@ -360,10 +362,10 @@
             )
 
         def arrived(s, q):
-            return spread(1 + s, s, q, slots.at[s], beside)
+            return spread(1 + s, s, q, slots.at[s], beside, spread_recv.at[s, q])
 
         def sideways(s, q):
-            return spread(3 + s, 2 + s, q, slots.at[s], across)
+            return spread(3 + s, 2 + s, q, slots.at[s], across, rest_recv.at[s])
 
         def back_x(p):
             return remote(
@@ -385,7 +387,7 @@
         def cross_corner(p):
             return remote(
                 other_pair.at[p, upper, :], from_corner.at[p], near_send.at[0],
-                near_recv.at[2, p], across,
+                near_recv.at[2, group(p)], across,
             )
 
         for q in range(batches):
@@ -410,10 +412,9 @@
         hidden = hidden_of(0, True)
         for p in range(pieces):
             keep[p] = down(hidden, p)
-        for q in range(batches):
-            for s in range(2):
-                with scope(f"w_G{s}{q}"):
-                    sideways(s, q).wait_recv()
+        for s in range(2):
+            with scope(f"w_G{s}"):
+                whole(slots.at[2 + s], rest_recv.at[s]).wait()
         hidden = hidden_of(2, False)
         for p in range(pieces):
             first_out[p] = down(hidden, p).astype(jnp.bfloat16)
@@ -438,15 +439,18 @@
             with scope("w_i1"):
                 whole(own_pair, pair_recv.at[0]).wait()
             for p in range(pieces):
-                with scope(f"w_iz{p}"):
-                    whole(from_beside.at[p], near_recv.at[0, p]).wait()
+                if p == 0:
+                    with scope("w_iz"):
+                        for g in range(groups):
+                            grouped(from_beside, 0, g).wait()
                 sums = own_pair[p, upper, :].astype(jnp.float32)
                 sums = sums + from_beside[p, upper, :].astype(jnp.float32)
                 to_cross[p] = sums.astype(jnp.bfloat16)
                 cross(p, to_cross.at[p]).start()
             for p in range(pieces):
-                with scope(f"w_ic{p}"):
-                    cross_corner(p).wait_recv()
+                if p * groups % pieces == 0:
+                    with scope(f"w_ic{p}"):
+                        grouped(from_corner, 2, group(p)).wait()
                 sums = other_pair[p, lower, :].astype(jnp.float32)
                 sums = sums + from_corner[p].astype(jnp.float32)
                 to_merge[p] = sums.astype(jnp.bfloat16)
@@ -458,13 +462,14 @@
                 whole(own_pair.at[:, lower, :], pair_recv.at[0]).wait()
 
         for p in range(pieces):
-            with scope(f"w_xA{p}"):
-                whole(from_across.at[p], near_recv.at[1, p]).wait()
-
-            @pl.when(is_outer)
-            def _():
-                with scope(f"w_oz{p}"):
-                    whole(from_beside.at[p, lower, :], near_recv.at[0, p]).wait()
+            if p * groups % pieces == 0:
+                with scope(f"w_xA{p}"):
+                    grouped(from_across, 1, group(p)).wait()
+
+                @pl.when(is_outer)
+                def _():
+                    with scope(f"w_oz{p}"):
+                        grouped(from_beside.at[:, lower, :], 0, group(p)).wait()
 
             total = held[:, part(p)].astype(jnp.float32)
             total = total + own_pair[p, lower, :].astype(jnp.float32)
@@ -474,9 +479,8 @@
                 with scope(f"w_bz{s}{p}"):
                     came_z(s, p).wait()
                 total = total + shares[s] * second_in[p, (lower, upper)[s], :].astype(jnp.float32)
-            final[:, part(p)] = total.astype(jnp.bfloat16)
+            out_ref[:, part(p)] = total.astype(jnp.bfloat16)
             give(p).start()
-            stay(p).start()
         whole(own, spread_send.at[0]).wait()
         for s in range(2):
             whole(slots.at[s], spread_send.at[3 + s]).wait()
@@ -494,8 +498,7 @@
         for swap in swaps:
             swap.wait_send()
         with scope("w_end"):
-            whole(final, give_send).wait()
-            whole(final, keep_sem).wait()
+            whole(out_ref, give_send).wait()
 
 
 def dense_layer(tokens, gain, route_ids, route_weights, w_gate, w_up, w_down):
@@ -504,18 +507,19 @@
     batches = rows // 16
     pieces = 6
     width = features // pieces
-    hbm = pl.BlockSpec(memory_space=pl.ANY)
+    hbm = pl.BlockSpec(memory_space=pltpu.HBM)
     half = jnp.bfloat16
     dma = pltpu.SemaphoreType.DMA
     ids = route_ids.T
     weights = route_weights.T
+    operands = (tokens, gain, ids, weights, w_gate, w_up, w_down)
     travel = pltpu.VMEM((pieces, 2 * rows, width), half)
     single = pltpu.VMEM((pieces, rows, width), half)
     return pl.pallas_call(
         dense_kernel,
-        out_shape=jax.ShapeDtypeStruct(tokens.shape, tokens.dtype),
+        out_shape=pltpu.VMEM(tokens.shape, tokens.dtype),
         in_specs=[hbm] * 7,
-        out_specs=hbm,
+        out_specs=pl.BlockSpec(memory_space=pltpu.VMEM),
         scratch_shapes=[
             pltpu.VMEM((rows, features), half),
             pltpu.VMEM((features,), jnp.float32),
@@ -531,7 +535,6 @@
         + [travel] * 7
         + [single] * 4
         + [
-            pltpu.VMEM((rows, features), half),
             pltpu.VMEM(weights.shape, jnp.float32),
             pltpu.VMEM((3, *weights.shape), jnp.float32),
             dma((4,)),
@@ -541,20 +544,20 @@
             dma((3,)),
             dma((3,)),
             dma((5,)),
-            dma((4, batches)),
+            dma((2, batches)),
+            dma((2,)),
             dma((2,)),
             dma((3, pieces)),
             dma((4,)),
             dma((2,)),
-            dma((3, pieces)),
-            dma,
+            dma((3, 2)),
             dma,
             dma,
         ],
         compiler_params=pltpu.CompilerParams(
-            collective_id=0, has_side_effects=True, vmem_limit_bytes=66_000_000
+            collective_id=0, has_side_effects=True, vmem_limit_bytes=40_000_000
         ),
-    )(tokens, gain, ids, weights, w_gate, w_up, w_down)
+    )(*(pltpu.with_memory_space_constraint(array, pltpu.HBM) for array in operands))
 
 
 def route_tables(chosen_ids, chosen_weights, expert_count, slot_room):

time: 32.1 us -> 31 us (0.966)
  local copies, waits for them, and re-layouts: 1.62 us -> 0.68 us
    unnamed x1, local copies, waits for them, and re-layouts: 1.62 us -> 0.68 us
where the time goes in v3:
time: 31 us; the launch traced here: 30.8 us
  Pallas kernels  30.1 us (97%)
  local copies, waits for them, and re-layouts  0.68 us (2%)
    pallas_call x1, Pallas kernels, dense_layer(): pl.pallas_call(dense_kernel, out_shape=pltpu.VMEM(tokens.shape, tokens.dt...  30.1 us
    unnamed x1, local copies, waits for them, and re-layouts  0.68 us

profile of v3, /device:TPU:0, one launch (start us, length us, event | category | flops | bytes accessed | tf_op | source)
XLA Modules:
  0.0 30.8 jit_solution(13245419743734085932)
XLA Ops:
  0.0 30.1 %shard_map.73 = bf16[64,1536]{1,0:T(8,128)(2,1)S(1)} custom-call(bf16[64,1536]{1,0:T(8,128)(2,1)} %tokens_ref.1, f32[1536]{0:T(1024)} %gain_ref.1, s32[4,64]{1,0:T(4,128)} %bitcast.2, f32[4,64]{1,0:T(4,128)} %bitcast.3, bf16[1,1536,384]{2,1,0:T(8,128)(2,1)} %gate_ref.1, bf16[1,1536,384]{2,1,0:T(8,128)(2,1)} %up_ref.1, bf16[1,384,1536]{2,1,0:T(8,128)(2,1)} %down_ref.1), custom_call_target="tpu_custom_call" | custom-call | tf_op jit(solution)/shard_map/pallas_call | solution.py:518
  30.2 0.7 %copy.9 = bf16[64,1536]{1,0:T(8,128)(2,1)} copy(bf16[64,1536]{1,0:T(8,128)(2,1)S(1)} %shard_map.73) | data formatting | bytes 393216

commit v4 on v3

--- a/solution.py
+++ b/solution.py
@@ -36,12 +36,9 @@
     second_out,
     second_in,
     own_pair,
-    other_pair,
     from_beside,
     from_across,
-    from_corner,
     to_cross,
-    to_merge,
     line_out,
     line_in,
     small_sem,
@@ -222,17 +219,6 @@
     lower, upper = pl.ds(0, rows), pl.ds(rows, rows)
     both_halves = pl.ds(0, 2 * rows)
 
-    def cross(p, src):
-        return remote(
-            src, from_across.at[p], near_send.at[2], near_recv.at[1, group(p)], on(across, 1)
-        )
-
-    def along(p, src, rows_there):
-        return remote(
-            src, from_beside.at[p, rows_there, :], near_send.at[1], near_recv.at[0, group(p)],
-            on(beside, 1),
-        )
-
     @pl.when(core == 0)
     def _():
         def to_across(q):
@@ -246,6 +232,12 @@
 
         def on_to_across(q):
             return spread(3, 3, q, slots.at[2], across, rest_recv.at[0])
+
+        def along(p):
+            return remote(
+                second_out.at[p], from_beside.at[p], near_send.at[1], near_recv.at[0, group(p)],
+                on(beside, 1),
+            )
 
         def line_to(i):
             return remote(
@@ -297,21 +289,19 @@
         for p in range(pieces):
             first_out[p] = (down(hidden, p) * scales).astype(jnp.bfloat16)
 
-        def hand_pair(src, dst, i):
-            return remote(src, dst, near_send.at[3 * i], pair_recv.at[i], sibling)
+        def hand_pair(p):
+            return remote(
+                first_out.at[p], own_pair.at[p], near_send.at[0], pair_recv, sibling
+            )
+
+        for p in range(pieces):
+            hand_pair(p).start()
 
         @pl.when(is_inner)
         def _():
-            for p in range(pieces):
-                hand_pair(first_out.at[p], own_pair.at[p], 0).start()
             for q in range(batches):
                 with scope(f"w_P{q}"):
                     to_beside(q).wait_recv()
-
-        @pl.when(is_outer)
-        def _():
-            for p in range(pieces):
-                hand_pair(first_out.at[p, lower, :], own_pair.at[p, lower, :], 0).start()
 
         with scope("w_D"):
             whole(slots.at[3], rest_recv.at[0]).wait()
@@ -320,14 +310,7 @@
         for p in range(pieces):
             second_out[p] = (down(hidden, p) * scales).astype(jnp.bfloat16)
 
-            @pl.when(is_inner)
-            def _():
-                hand_pair(second_out.at[p], other_pair.at[p], 1).start()
-
-            @pl.when(is_outer)
-            def _():
-                along(p, second_out.at[p], both_halves).start()
-
+            along(p).start()
         whole(slots.at[0], spread_send.at[0]).wait()
         whole(slots.at[0], spread_send.at[1]).wait()
         for i in range(3):
@@ -335,19 +318,11 @@
 
         @pl.when(is_outer)
         def _():
-            for p in range(pieces):
-                cross(p, first_out.at[p, upper, :]).start()
             whole(slots.at[1], spread_send.at[2]).wait()
             whole(slots.at[2], spread_send.at[3]).wait()
-            whole(first_out.at[:, lower, :], near_send.at[0]).wait()
-            whole(second_out, near_send.at[1]).wait()
-            whole(first_out.at[:, upper, :], near_send.at[2]).wait()
-
-        @pl.when(is_inner)
-        def _():
-            whole(first_out, near_send.at[0]).wait()
-            whole(second_out, near_send.at[3]).wait()
-
+
+        whole(first_out, near_send.at[0]).wait()
+        whole(second_out, near_send.at[1]).wait()
         for swap in swaps:
             swap.wait_send()
         with scope("w_give"):
@@ -384,10 +359,10 @@
         def came_z(s, p):
             return whole(second_in.at[p, (lower, upper)[s], :], back_recv.at[1 + s, p])
 
-        def cross_corner(p):
+        def cross(p):
             return remote(
-                other_pair.at[p, upper, :], from_corner.at[p], near_send.at[0],
-                near_recv.at[2, group(p)], across,
+                to_cross.at[p], from_across.at[p], near_send.at[2], near_recv.at[1, group(p)],
+                across,
             )
 
         for q in range(batches):
@@ -420,57 +395,29 @@
             first_out[p] = down(hidden, p).astype(jnp.bfloat16)
             back_x(p).start()
 
-        @pl.when(is_inner)
-        def _():
-            with scope("w_i2"):
-                whole(other_pair, pair_recv.at[1]).wait()
-            for p in range(pieces):
-                cross_corner(p).start()
-
+        span = pieces // groups
         for p in range(pieces):
             with scope(f"w_bx{p}"):
                 back_x(p).wait_recv()
             second_out[p] = (keep[p] + first_in[p].astype(jnp.float32)).astype(jnp.bfloat16)
             for s in range(2):
                 back_z(s, p).start()
-
-        @pl.when(is_inner)
-        def _():
-            with scope("w_i1"):
-                whole(own_pair, pair_recv.at[0]).wait()
-            for p in range(pieces):
-                if p == 0:
-                    with scope("w_iz"):
-                        for g in range(groups):
-                            grouped(from_beside, 0, g).wait()
-                sums = own_pair[p, upper, :].astype(jnp.float32)
-                sums = sums + from_beside[p, upper, :].astype(jnp.float32)
-                to_cross[p] = sums.astype(jnp.bfloat16)
-                cross(p, to_cross.at[p]).start()
-            for p in range(pieces):
-                if p * groups % pieces == 0:
-                    with scope(f"w_ic{p}"):
-                        grouped(from_corner, 2, group(p)).wait()
-                sums = other_pair[p, lower, :].astype(jnp.float32)
-                sums = sums + from_corner[p].astype(jnp.float32)
-                to_merge[p] = sums.astype(jnp.bfloat16)
-                along(p, to_merge.at[p], lower).start()
-
-        @pl.when(is_outer)
-        def _():
-            with scope("w_o1"):
-                whole(own_pair.at[:, lower, :], pair_recv.at[0]).wait()
-
+            g = p - (pieces - groups)
+            if g < 0:
+                continue
+            with scope(f"w_be{g}"):
+                if g == 0:
+                    whole(own_pair, pair_recv).wait()
+                grouped(from_beside, 0, g).wait()
+            for i in range(g * span, g * span + span):
+                sums = own_pair[i, upper, :].astype(jnp.float32)
+                sums = sums + from_beside[i, upper, :].astype(jnp.float32)
+                to_cross[i] = sums.astype(jnp.bfloat16)
+                cross(i).start()
         for p in range(pieces):
-            if p * groups % pieces == 0:
+            if p % span == 0:
                 with scope(f"w_xA{p}"):
                     grouped(from_across, 1, group(p)).wait()
-
-                @pl.when(is_outer)
-                def _():
-                    with scope(f"w_oz{p}"):
-                        grouped(from_beside.at[:, lower, :], 0, group(p)).wait()
-
             total = held[:, part(p)].astype(jnp.float32)
             total = total + own_pair[p, lower, :].astype(jnp.float32)
             total = total + from_beside[p, lower, :].astype(jnp.float32)
@@ -486,14 +433,12 @@
             whole(slots.at[s], spread_send.at[3 + s]).wait()
         whole(first_out, back_send.at[0]).wait()
         whole(second_out, back_send.at[1]).wait()
+        whole(to_cross, near_send.at[2]).wait()
 
         @pl.when(is_inner)
         def _():
             for s in range(2):
                 whole(slots.at[s], spread_send.at[1 + s]).wait()
-            whole(from_corner, near_send.at[0]).wait()
-            whole(to_merge, near_send.at[1]).wait()
-            whole(to_cross, near_send.at[2]).wait()
 
         for swap in swaps:
             swap.wait_send()
@@ -532,8 +477,8 @@
             pltpu.VMEM((4, rows, features), half),
             pltpu.VMEM((pieces, 2 * rows, width), jnp.float32),
         ]
-        + [travel] * 7
-        + [single] * 4
+        + [travel] * 6
+        + [single] * 2
         + [
             pltpu.VMEM(weights.shape, jnp.float32),
             pltpu.VMEM((3, *weights.shape), jnp.float32),
@@ -548,9 +493,9 @@
             dma((2,)),
             dma((2,)),
             dma((3, pieces)),
-            dma((4,)),
-            dma((2,)),
-            dma((3, 2)),
+            dma((3,)),
+            dma,
+            dma((2, 2)),
             dma,
             dma,
         ],

time: 31 us -> 29.8 us (0.961)
  Pallas kernels: 30.1 us -> 29 us
    pallas_call x1, Pallas kernels: 30.1 us -> 29 us  [dense_layer(): pl.pallas_call(dense_kernel, out_shape=pltpu.VMEM(tokens.shape, tokens.dt...]
where the time goes in v4:
time: 29.8 us; the launch traced here: 29.7 us
  Pallas kernels  29 us (97%)
  local copies, waits for them, and re-layouts  0.68 us (2%)
    pallas_call x1, Pallas kernels, dense_layer(): pl.pallas_call(dense_kernel, out_shape=pltpu.VMEM(tokens.shape, tokens.dt...  29 us
    unnamed x1, local copies, waits for them, and re-layouts  0.68 us

profile of v4, /device:TPU:0, one launch (start us, length us, event | category | flops | bytes accessed | tf_op | source)
XLA Modules:
  0.0 29.7 jit_solution(2507604506443275250)
XLA Ops:
  0.0 29.0 %shard_map.73 = bf16[64,1536]{1,0:T(8,128)(2,1)S(1)} custom-call(bf16[64,1536]{1,0:T(8,128)(2,1)} %tokens_ref.1, f32[1536]{0:T(1024)} %gain_ref.1, s32[4,64]{1,0:T(4,128)} %bitcast.2, f32[4,64]{1,0:T(4,128)} %bitcast.3, bf16[1,1536,384]{2,1,0:T(8,128)(2,1)} %gate_ref.1, bf16[1,1536,384]{2,1,0:T(8,128)(2,1)} %up_ref.1, bf16[1,384,1536]{2,1,0:T(8,128)(2,1)} %down_ref.1), custom_call_target="tpu_custom_call" | custom-call | tf_op jit(solution)/shard_map/pallas_call | solution.py:463
  29.0 0.7 %copy.9 = bf16[64,1536]{1,0:T(8,128)(2,1)} copy(bf16[64,1536]{1,0:T(8,128)(2,1)S(1)} %shard_map.73) | data formatting | bytes 393216

commit v5 on v4

--- a/solution.py
+++ b/solution.py
@@ -99,15 +99,19 @@
         return {**peer, "tensor": which}
 
     near_peers = [across, beside, corner, sibling]
-    far_peers = [across, beside, *far, sibling]
+    far_peers = [across, beside, far[0], sibling]
 
     @pl.when(core == 0)
     def _():
-        greet(near_peers)
+        greet([*near_peers, on(across, 1), on(beside, 1)])
 
     @pl.when(core == 1)
     def _():
-        greet([*far_peers, on(across, 0), on(beside, 0)])
+        greet([across, beside, sibling, on(across, 0), on(beside, 0)])
+
+        @pl.when(is_inner)
+        def _():
+            greet(far)
 
     smalls = [
         pltpu.make_async_copy(src, dst, small_sem.at[i])
@@ -221,11 +225,11 @@
 
     @pl.when(core == 0)
     def _():
-        def to_across(q):
-            return spread(0, 1, q, slots.at[0], across, spread_recv.at[0, q])
-
-        def to_beside(q):
-            return spread(1, 2, q, slots.at[0], beside, spread_recv.at[1, q])
+        def across_came(q):
+            return whole(slots.at[1, rows_of(q), :], spread_recv.at[0, q])
+
+        def beside_came(q):
+            return whole(slots.at[2, rows_of(q), :], spread_recv.at[1, q])
 
         def on_to_beside(q):
             return spread(2, 3, q, slots.at[1], beside, rest_recv.at[0])
@@ -241,7 +245,7 @@
 
         def line_to(i):
             return remote(
-                line_out, line_in.at[i], line_send.at[i], line_recv.at[i],
+                line_out, line_in.at[i], line_send, line_recv,
                 (across, beside, corner)[i],
             )
 
@@ -253,20 +257,17 @@
             pl.semaphore_wait(barrier, len(near_peers) + 2)
         for i in range(3):
             line_to(i).start()
-        for q in range(batches):
-            to_across(q).start()
-            to_beside(q).start()
         for swap in swaps:
             swap.start()
         for q in range(batches):
             with scope(f"w_A{q}"):
-                to_across(q).wait_recv()
+                across_came(q).wait()
 
             @pl.when(is_outer)
             def _():
                 on_to_beside(q).start()
                 with scope(f"w_Po{q}"):
-                    to_beside(q).wait_recv()
+                    beside_came(q).wait()
                 on_to_across(q).start()
 
         def share(table):
@@ -281,8 +282,7 @@
 
         hidden = hidden_of(0, True)
         with scope("w_line"):
-            for i in range(3):
-                line_to(i).wait_recv()
+            whole(line_in, line_recv).wait()
         own_share = share(line_out[...])
         shares = [share(line_in[i]) for i in range(3)]
         scales = jnp.concatenate([own_share, shares[0]], axis=0)
@@ -301,7 +301,7 @@
         def _():
             for q in range(batches):
                 with scope(f"w_P{q}"):
-                    to_beside(q).wait_recv()
+                    beside_came(q).wait()
 
         with scope("w_D"):
             whole(slots.at[3], rest_recv.at[0]).wait()
@@ -311,10 +311,7 @@
             second_out[p] = (down(hidden, p) * scales).astype(jnp.bfloat16)
 
             along(p).start()
-        whole(slots.at[0], spread_send.at[0]).wait()
-        whole(slots.at[0], spread_send.at[1]).wait()
-        for i in range(3):
-            line_to(i).wait_send()
+        whole(line_in, line_send).wait()
 
         @pl.when(is_outer)
         def _():
@@ -330,6 +327,18 @@
 
     @pl.when(core == 1)
     def _():
+        def near_x(q):
+            return remote(
+                own.at[rows_of(q), :], slots.at[1, rows_of(q), :], spread_send.at[5],
+                spread_recv.at[0, q], on(across, 0),
+            )
+
+        def near_z(q):
+            return remote(
+                own.at[rows_of(q), :], slots.at[2, rows_of(q), :], spread_send.at[6],
+                spread_recv.at[1, q], on(beside, 0),
+            )
+
         def outward(q):
             return remote(
                 own.at[rows_of(q), :], slots.at[my_far_slot, rows_of(q), :], spread_send.at[0],
@@ -367,10 +376,13 @@
 
         for q in range(batches):
             own[rows_of(q), :] = normed(q)
-        with scope("w_bar"):
-            pl.semaphore_wait(barrier, len(far_peers))
+            if q == 0:
+                with scope("w_bar"):
+                    pl.semaphore_wait(barrier, len(far_peers) + 2)
+            outward(q).start()
+            near_x(q).start()
         for q in range(batches):
-            outward(q).start()
+            near_z(q).start()
         for swap in swaps:
             swap.start()
         shares = [column(line_of(spot)) for spot in far_spots]
@@ -400,7 +412,7 @@
             with scope(f"w_bx{p}"):
                 back_x(p).wait_recv()
             second_out[p] = (keep[p] + first_in[p].astype(jnp.float32)).astype(jnp.bfloat16)
-            for s in range(2):
+            for s in (1, 0):
                 back_z(s, p).start()
             g = p - (pieces - groups)
             if g < 0:
@@ -428,7 +440,8 @@
                 total = total + shares[s] * second_in[p, (lower, upper)[s], :].astype(jnp.float32)
             out_ref[:, part(p)] = total.astype(jnp.bfloat16)
             give(p).start()
-        whole(own, spread_send.at[0]).wait()
+        for lane in (0, 5, 6):
+            whole(own, spread_send.at[lane]).wait()
         for s in range(2):
             whole(slots.at[s], spread_send.at[3 + s]).wait()
         whole(first_out, back_send.at[0]).wait()
@@ -486,9 +499,9 @@
             dma((3,)),
             dma((3,)),
             dma((3,)),
-            dma((3,)),
-            dma((3,)),
-            dma((5,)),
+            dma,
+            dma,
+            dma((7,)),
             dma((2, batches)),
             dma((2,)),
             dma((2,)),

time: 29.8 us -> 29.3 us (0.983)
  Pallas kernels: 29 us -> 28.4 us
    pallas_call x1, Pallas kernels: 29 us -> 28.4 us  [dense_layer(): pl.pallas_call(dense_kernel, out_shape=pltpu.VMEM(tokens.shape, tokens.dt...]
where the time goes in v5:
time: 29.3 us; the launch traced here: 29.1 us
  Pallas kernels  28.4 us (97%)
  local copies, waits for them, and re-layouts  0.68 us (2%)
    pallas_call x1, Pallas kernels, dense_layer(): pl.pallas_call(dense_kernel, out_shape=pltpu.VMEM(tokens.shape, tokens.dt...  28.4 us
    unnamed x1, local copies, waits for them, and re-layouts  0.68 us

profile of v5, /device:TPU:0, one launch (start us, length us, event | category | flops | bytes accessed | tf_op | source)
XLA Modules:
  0.0 29.1 jit_solution(7058094215548728640)
XLA Ops:
  0.0 28.4 %shard_map.73 = bf16[64,1536]{1,0:T(8,128)(2,1)S(1)} custom-call(bf16[64,1536]{1,0:T(8,128)(2,1)} %tokens_ref.1, f32[1536]{0:T(1024)} %gain_ref.1, s32[4,64]{1,0:T(4,128)} %bitcast.2, f32[4,64]{1,0:T(4,128)} %bitcast.3, bf16[1,1536,384]{2,1,0:T(8,128)(2,1)} %gate_ref.1, bf16[1,1536,384]{2,1,0:T(8,128)(2,1)} %up_ref.1, bf16[1,384,1536]{2,1,0:T(8,128)(2,1)} %down_ref.1), custom_call_target="tpu_custom_call" | custom-call | tf_op jit(solution)/shard_map/pallas_call | solution.py:476
  28.4 0.7 %copy.9 = bf16[64,1536]{1,0:T(8,128)(2,1)} copy(bf16[64,1536]{1,0:T(8,128)(2,1)S(1)} %shard_map.73) | data formatting | bytes 393216

commit v6 on v5

--- a/solution.py
+++ b/solution.py
@@ -1,3 +1,5 @@
+import functools
+
 import jax
 import jax.numpy as jnp
 from jax import lax
@@ -43,20 +45,13 @@
     line_in,
     small_sem,
     load_sem,
-    swap_send,
     swap_recv,
-    line_send,
-    line_recv,
-    spread_send,
+    sent,
     spread_recv,
     rest_recv,
-    back_send,
-    back_recv,
-    near_send,
+    done_recv,
+    near_recv,
     pair_recv,
-    near_recv,
-    give_send,
-    give_recv,
 ):
     me = lax.axis_index("expert")
     core = lax.axis_index("tensor")
@@ -83,7 +78,7 @@
 
     rows, features = own.shape
     cols = gate_ref.shape[2]
-    batches = spread_recv.shape[1]
+    batches = rows // 16
     groups = near_recv.shape[1]
     batch = rows // batches
     pieces, _, width = keep.shape
@@ -145,7 +140,7 @@
         )
 
     swaps = [
-        remote(src, dst(1), swap_send.at[i], swap_recv.at[i], sibling)
+        remote(src, dst(1), sent.at[3 + i // 2], swap_recv.at[i], sibling)
         for i, (src, dst) in enumerate(pairs)
     ]
 
@@ -159,13 +154,11 @@
         smalls[0].wait()
         smalls[1].wait()
 
-    def normed(q):
-        resident = held[rows_of(q), :].astype(jnp.float32)
+    def normed():
+        resident = held[...].astype(jnp.float32)
         inv_rms = lax.rsqrt(jnp.mean(resident * resident, axis=1, keepdims=True) + 1e-05)
         return (resident * inv_rms * gain[...].reshape(1, -1)).astype(jnp.bfloat16)
 
-    smalls[2].wait()
-    smalls[3].wait()
     lanes = line_out.shape[1]
     spots = line_out.shape[0]
     spot_ids = lax.broadcasted_iota(jnp.int32, (rows, rows), 0)
@@ -203,15 +196,22 @@
 
     def give(p):
         there = out_ref.at[:, part(p)]
-        return remote(there, there, give_send, give_recv, sibling)
+        return remote(there, there, sent.at[5], done_recv.at[1], sibling)
 
     def whole(ref, sem):
         return pltpu.make_async_copy(ref, ref, sem)
 
-    def spread(lane, slot, q, src, peer, recv):
+    def spread(slot, q, src, peer, recv):
         return remote(
-            src.at[rows_of(q), :], slots.at[slot, rows_of(q), :], spread_send.at[lane], recv, peer
+            src.at[rows_of(q), :], slots.at[slot, rows_of(q), :], sent.at[0], recv, peer
         )
+
+    def blocks_sent(count):
+        whole(wd.at[pl.ds(0, count * rows), :], sent.at[0]).wait()
+
+    def swaps_sent():
+        whole(wg, sent.at[3]).wait()
+        swaps[2].wait_send()
 
     def group(p):
         return p * groups // pieces
@@ -232,25 +232,26 @@
             return whole(slots.at[2, rows_of(q), :], spread_recv.at[1, q])
 
         def on_to_beside(q):
-            return spread(2, 3, q, slots.at[1], beside, rest_recv.at[0])
+            return spread(3, q, slots.at[1], beside, rest_recv)
 
         def on_to_across(q):
-            return spread(3, 3, q, slots.at[2], across, rest_recv.at[0])
+            return spread(3, q, slots.at[2], across, rest_recv)
 
         def along(p):
             return remote(
-                second_out.at[p], from_beside.at[p], near_send.at[1], near_recv.at[0, group(p)],
+                second_out.at[p], from_beside.at[p], sent.at[2], near_recv.at[0, group(p)],
                 on(beside, 1),
             )
 
         def line_to(i):
             return remote(
-                line_out, line_in.at[i], line_send, line_recv,
+                line_out, line_in.at[i], sent.at[5], done_recv.at[0],
                 (across, beside, corner)[i],
             )
 
-        for q in range(batches):
-            slots[0, rows_of(q), :] = normed(q)
+        slots[0] = normed()
+        smalls[2].wait()
+        smalls[3].wait()
         for spot in range(spots):
             line_out[spot : spot + 1, :] = line_of(spot)
         with scope("w_bar"):
@@ -282,7 +283,7 @@
 
         hidden = hidden_of(0, True)
         with scope("w_line"):
-            whole(line_in, line_recv).wait()
+            whole(line_in, done_recv.at[0]).wait()
         own_share = share(line_out[...])
         shares = [share(line_in[i]) for i in range(3)]
         scales = jnp.concatenate([own_share, shares[0]], axis=0)
@@ -291,7 +292,7 @@
 
         def hand_pair(p):
             return remote(
-                first_out.at[p], own_pair.at[p], near_send.at[0], pair_recv, sibling
+                first_out.at[p], own_pair.at[p], sent.at[1], pair_recv, sibling
             )
 
         for p in range(pieces):
@@ -304,119 +305,114 @@
                     beside_came(q).wait()
 
         with scope("w_D"):
-            whole(slots.at[3], rest_recv.at[0]).wait()
+            whole(slots.at[3], rest_recv).wait()
         hidden = hidden_of(2, False)
         scales = jnp.concatenate([shares[1], shares[2]], axis=0)
         for p in range(pieces):
             second_out[p] = (down(hidden, p) * scales).astype(jnp.bfloat16)
 
             along(p).start()
-        whole(line_in, line_send).wait()
+        whole(line_in, sent.at[5]).wait()
 
         @pl.when(is_outer)
         def _():
-            whole(slots.at[1], spread_send.at[2]).wait()
-            whole(slots.at[2], spread_send.at[3]).wait()
-
-        whole(first_out, near_send.at[0]).wait()
-        whole(second_out, near_send.at[1]).wait()
-        for swap in swaps:
-            swap.wait_send()
+            blocks_sent(2)
+
+        whole(first_out, sent.at[1]).wait()
+        whole(second_out, sent.at[2]).wait()
+        swaps_sent()
         with scope("w_give"):
-            whole(out_ref, give_recv).wait()
+            whole(out_ref, done_recv.at[1]).wait()
 
     @pl.when(core == 1)
     def _():
         def near_x(q):
             return remote(
-                own.at[rows_of(q), :], slots.at[1, rows_of(q), :], spread_send.at[5],
+                own.at[rows_of(q), :], slots.at[1, rows_of(q), :], sent.at[0],
                 spread_recv.at[0, q], on(across, 0),
             )
 
         def near_z(q):
             return remote(
-                own.at[rows_of(q), :], slots.at[2, rows_of(q), :], spread_send.at[6],
+                own.at[rows_of(q), :], slots.at[2, rows_of(q), :], sent.at[0],
                 spread_recv.at[1, q], on(beside, 0),
             )
 
         def outward(q):
             return remote(
-                own.at[rows_of(q), :], slots.at[my_far_slot, rows_of(q), :], spread_send.at[0],
+                own.at[rows_of(q), :], slots.at[my_far_slot, rows_of(q), :], sent.at[0],
                 spread_recv.at[my_far_slot, q], far[0],
             )
 
         def arrived(s, q):
-            return spread(1 + s, s, q, slots.at[s], beside, spread_recv.at[s, q])
+            return spread(s, q, slots.at[s], beside, spread_recv.at[s, q])
 
         def sideways(s, q):
-            return spread(3 + s, 2 + s, q, slots.at[s], across, rest_recv.at[s])
-
-        def back_x(p):
-            return remote(
-                first_out.at[p], first_in.at[p], back_send.at[0], back_recv.at[0, p], across
+            return spread(2 + s, q, slots.at[s], across, rest_recv)
+
+        def back_x(s, p):
+            rows_there = (lower, upper)[s]
+            return remote(
+                first_out.at[p, rows_there, :], first_in.at[p, rows_there, :], sent.at[1],
+                spread_recv.at[s, p], across,
             )
 
         def back_z(s, p):
             return remote(
                 second_out.at[p, (lower, upper)[s], :],
                 second_in.at[p, pl.ds(pl.multiple_of(my_far_slot * rows, rows), rows), :],
-                back_send.at[1],
-                back_recv.at[1 + my_far_slot, p],
+                sent.at[1],
+                done_recv.at[p],
                 far[s],
             )
 
-        def came_z(s, p):
-            return whole(second_in.at[p, (lower, upper)[s], :], back_recv.at[1 + s, p])
+        def came_z(p):
+            return whole(second_in.at[p], done_recv.at[p])
 
         def cross(p):
             return remote(
-                to_cross.at[p], from_across.at[p], near_send.at[2], near_recv.at[1, group(p)],
+                to_cross.at[p], from_across.at[p], sent.at[2], near_recv.at[1, group(p)],
                 across,
             )
 
+        own[...] = normed()
+        with scope("w_bar"):
+            pl.semaphore_wait(barrier, len(far_peers) + 2)
         for q in range(batches):
-            own[rows_of(q), :] = normed(q)
-            if q == 0:
-                with scope("w_bar"):
-                    pl.semaphore_wait(barrier, len(far_peers) + 2)
             outward(q).start()
+        for q in range(batches):
             near_x(q).start()
         for q in range(batches):
             near_z(q).start()
         for swap in swaps:
             swap.start()
+        smalls[2].wait()
+        smalls[3].wait()
         shares = [column(line_of(spot)) for spot in far_spots]
-        for q in range(batches):
-            for s in range(2):
-                with scope(f"w_F{s}{q}"):
-                    arrived(s, q).wait_recv()
-
-                @pl.when(is_inner)
-                def _():
-                    arrived(s, q).start()
-
-                sideways(s, q).start()
+        order = [(0, 0)] + [(1, q) for q in range(batches)] + [(0, q) for q in range(1, batches)]
+        for s, q in order:
+            with scope(f"w_F{s}{q}"):
+                arrived(s, q).wait_recv()
+
+            @pl.when(is_inner)
+            def _():
+                arrived(s, q).start()
+
+            sideways(s, q).start()
         hidden = hidden_of(0, True)
         for p in range(pieces):
             keep[p] = down(hidden, p)
-        for s in range(2):
-            with scope(f"w_G{s}"):
-                whole(slots.at[2 + s], rest_recv.at[s]).wait()
+        with scope("w_G"):
+            whole(slots.at[pl.ds(2, 2)], rest_recv).wait()
         hidden = hidden_of(2, False)
         for p in range(pieces):
             first_out[p] = down(hidden, p).astype(jnp.bfloat16)
-            back_x(p).start()
+            for s in (1, 0):
+                back_x(s, p).start()
 
         span = pieces // groups
-        for p in range(pieces):
-            with scope(f"w_bx{p}"):
-                back_x(p).wait_recv()
-            second_out[p] = (keep[p] + first_in[p].astype(jnp.float32)).astype(jnp.bfloat16)
-            for s in (1, 0):
-                back_z(s, p).start()
-            g = p - (pieces - groups)
-            if g < 0:
-                continue
+
+        def merge(g):
             with scope(f"w_be{g}"):
                 if g == 0:
                     whole(own_pair, pair_recv).wait()
@@ -426,6 +422,20 @@
                 sums = sums + from_beside[i, upper, :].astype(jnp.float32)
                 to_cross[i] = sums.astype(jnp.bfloat16)
                 cross(i).start()
+
+        for p in range(pieces):
+            for s in (1, 0):
+                there = (lower, upper)[s]
+                with scope(f"w_bx{s}{p}"):
+                    back_x(s, p).wait_recv()
+                both = keep[p, there, :] + first_in[p, there, :].astype(jnp.float32)
+                second_out[p, there, :] = both.astype(jnp.bfloat16)
+                back_z(s, p).start()
+            for g in range(groups):
+                if p == pieces - groups + g:
+                    pl.when(is_inner)(functools.partial(merge, g))
+                if p == 1 + 2 * g:
+                    pl.when(is_outer)(functools.partial(merge, g))
         for p in range(pieces):
             if p % span == 0:
                 with scope(f"w_xA{p}"):
@@ -434,29 +444,26 @@
             total = total + own_pair[p, lower, :].astype(jnp.float32)
             total = total + from_beside[p, lower, :].astype(jnp.float32)
             total = total + from_across[p].astype(jnp.float32)
+            with scope(f"w_bz{p}"):
+                came_z(p).wait()
             for s in range(2):
-                with scope(f"w_bz{s}{p}"):
-                    came_z(s, p).wait()
                 total = total + shares[s] * second_in[p, (lower, upper)[s], :].astype(jnp.float32)
             out_ref[:, part(p)] = total.astype(jnp.bfloat16)
             give(p).start()
-        for lane in (0, 5, 6):
-            whole(own, spread_send.at[lane]).wait()
-        for s in range(2):
-            whole(slots.at[s], spread_send.at[3 + s]).wait()
-        whole(first_out, back_send.at[0]).wait()
-        whole(second_out, back_send.at[1]).wait()
-        whole(to_cross, near_send.at[2]).wait()
+        whole(keep, sent.at[1]).wait()
+        whole(to_cross, sent.at[2]).wait()
 
         @pl.when(is_inner)
         def _():
-            for s in range(2):
-                whole(slots.at[s], spread_send.at[1 + s]).wait()
-
-        for swap in swaps:
-            swap.wait_send()
+            blocks_sent(7)
+
+        @pl.when(is_outer)
+        def _():
+            blocks_sent(5)
+
+        swaps_sent()
         with scope("w_end"):
-            whole(out_ref, give_send).wait()
+            whole(out_ref, sent.at[5]).wait()
 
 
 def dense_layer(tokens, gain, route_ids, route_weights, w_gate, w_up, w_down):
@@ -498,18 +505,11 @@
             dma((4,)),
             dma((3,)),
             dma((3,)),
-            dma((3,)),
+            dma((6,)),
+            dma((2, max(batches, pieces))),
             dma,
-            dma,
-            dma((7,)),
-            dma((2, batches)),
-            dma((2,)),
-            dma((2,)),
-            dma((3, pieces)),
-            dma((3,)),
-            dma,
+            dma((pieces,)),
             dma((2, 2)),
-            dma,
             dma,
         ],
         compiler_params=pltpu.CompilerParams(

time: 29.3 us -> 27.9 us (0.952)
  Pallas kernels: 28.4 us -> 27.1 us
    pallas_call x1, Pallas kernels: 28.4 us -> 27.1 us  [dense_layer(): pl.pallas_call(dense_kernel, out_shape=pltpu.VMEM(tokens.shape, tokens.dt...]
where the time goes in v6:
time: 27.9 us; the launch traced here: 27.8 us
  Pallas kernels  27.1 us (97%)
  local copies, waits for them, and re-layouts  0.68 us (2%)
    pallas_call x1, Pallas kernels, dense_layer(): pl.pallas_call(dense_kernel, out_shape=pltpu.VMEM(tokens.shape, tokens.dt...  27.1 us
    unnamed x1, local copies, waits for them, and re-layouts  0.68 us

profile of v6, /device:TPU:0, one launch (start us, length us, event | category | flops | bytes accessed | tf_op | source)
XLA Modules:
  0.0 27.8 jit_solution(13738574435286381190)
XLA Ops:
  0.0 27.1 %shard_map.73 = bf16[64,1536]{1,0:T(8,128)(2,1)S(1)} custom-call(bf16[64,1536]{1,0:T(8,128)(2,1)} %tokens_ref.1, f32[1536]{0:T(1024)} %gain_ref.1, s32[4,64]{1,0:T(4,128)} %bitcast.2, f32[4,64]{1,0:T(4,128)} %bitcast.3, bf16[1,1536,384]{2,1,0:T(8,128)(2,1)} %gate_ref.1, bf16[1,1536,384]{2,1,0:T(8,128)(2,1)} %up_ref.1, bf16[1,384,1536]{2,1,0:T(8,128)(2,1)} %down_ref.1), custom_call_target="tpu_custom_call" | custom-call | tf_op jit(solution)/shard_map/pallas_call | solution.py:483
  27.1 0.7 %copy.9 = bf16[64,1536]{1,0:T(8,128)(2,1)} copy(bf16[64,1536]{1,0:T(8,128)(2,1)S(1)} %shard_map.73) | data formatting | bytes 393216

commit v7 on v6

--- a/solution.py
+++ b/solution.py
@@ -175,8 +175,8 @@
         loads[i].wait()
         swaps[i].wait_recv()
 
-    def hidden_of(first, fresh):
-        block = slots[pl.ds(first, 2)].reshape(2 * rows, features)
+    def hidden_of(first, count, fresh):
+        block = slots[pl.ds(first, count)].reshape(count * rows, features)
         if fresh:
             with scope("w_wg"):
                 ready(0)
@@ -220,8 +220,8 @@
         span = pieces // groups
         return whole(ref.at[pl.ds(g * span, span)], near_recv.at[i, g])
 
+    batched = (range(1), range(1, pieces // 2), range(pieces // 2, pieces))
     lower, upper = pl.ds(0, rows), pl.ds(rows, rows)
-    both_halves = pl.ds(0, 2 * rows)
 
     @pl.when(core == 0)
     def _():
@@ -232,14 +232,14 @@
             return whole(slots.at[2, rows_of(q), :], spread_recv.at[1, q])
 
         def on_to_beside(q):
-            return spread(3, q, slots.at[1], beside, rest_recv)
+            return spread(3, q, slots.at[1], beside, rest_recv.at[0])
 
         def on_to_across(q):
-            return spread(3, q, slots.at[2], across, rest_recv)
-
-        def along(p):
-            return remote(
-                second_out.at[p], from_beside.at[p], sent.at[2], near_recv.at[0, group(p)],
+            return spread(3, q, slots.at[2], across, rest_recv.at[0])
+
+        def along(p, half, recv):
+            return remote(
+                second_out.at[p, half, :], from_beside.at[p, half, :], sent.at[2], recv,
                 on(beside, 1),
             )
 
@@ -281,7 +281,7 @@
             )
             return column(own_line)
 
-        hidden = hidden_of(0, True)
+        hidden = hidden_of(0, 2, True)
         with scope("w_line"):
             whole(line_in, done_recv.at[0]).wait()
         own_share = share(line_out[...])
@@ -305,13 +305,16 @@
                     beside_came(q).wait()
 
         with scope("w_D"):
-            whole(slots.at[3], rest_recv).wait()
-        hidden = hidden_of(2, False)
+            whole(slots.at[3], rest_recv.at[0]).wait()
+        hidden = hidden_of(2, 2, False)
         scales = jnp.concatenate([shares[1], shares[2]], axis=0)
+        for batch_of in batched:
+            for p in batch_of:
+                second_out[p] = (down(hidden, p) * scales).astype(jnp.bfloat16)
+            for p in batch_of:
+                along(p, upper, near_recv.at[0, group(p)]).start()
         for p in range(pieces):
-            second_out[p] = (down(hidden, p) * scales).astype(jnp.bfloat16)
-
-            along(p).start()
+            along(p, lower, near_recv.at[2, 0]).start()
         whole(line_in, sent.at[5]).wait()
 
         @pl.when(is_outer)
@@ -348,7 +351,7 @@
             return spread(s, q, slots.at[s], beside, spread_recv.at[s, q])
 
         def sideways(s, q):
-            return spread(2 + s, q, slots.at[s], across, rest_recv)
+            return spread(3 - s, q, slots.at[s], across, rest_recv.at[s])
 
         def back_x(s, p):
             rows_there = (lower, upper)[s]
@@ -389,8 +392,7 @@
         smalls[2].wait()
         smalls[3].wait()
         shares = [column(line_of(spot)) for spot in far_spots]
-        order = [(0, 0)] + [(1, q) for q in range(batches)] + [(0, q) for q in range(1, batches)]
-        for s, q in order:
+        for s, q in [(1, q) for q in range(batches)] + [(0, q) for q in range(batches)]:
             with scope(f"w_F{s}{q}"):
                 arrived(s, q).wait_recv()
 
@@ -399,43 +401,50 @@
                 arrived(s, q).start()
 
             sideways(s, q).start()
-        hidden = hidden_of(0, True)
+        with scope("w_G1"):
+            whole(slots.at[2], rest_recv.at[1]).wait()
+        hidden = hidden_of(0, 3, True)
+        for batch_of in batched:
+            for p in batch_of:
+                first_out[p, upper, :] = down(hidden[2 * rows :], p).astype(jnp.bfloat16)
+            for p in batch_of:
+                back_x(1, p).start()
+        with scope("w_G0"):
+            whole(slots.at[3], rest_recv.at[0]).wait()
+        late_hidden = hidden_of(3, 1, False)
+        for batch_of in batched:
+            for p in batch_of:
+                first_out[p, lower, :] = down(late_hidden, p).astype(jnp.bfloat16)
+            for p in batch_of:
+                back_x(0, p).start()
         for p in range(pieces):
-            keep[p] = down(hidden, p)
-        with scope("w_G"):
-            whole(slots.at[pl.ds(2, 2)], rest_recv).wait()
-        hidden = hidden_of(2, False)
-        for p in range(pieces):
-            first_out[p] = down(hidden, p).astype(jnp.bfloat16)
-            for s in (1, 0):
-                back_x(s, p).start()
-
+            keep[p] = down(hidden[: 2 * rows], p)
         span = pieces // groups
 
         def merge(g):
             with scope(f"w_be{g}"):
                 if g == 0:
                     whole(own_pair, pair_recv).wait()
-                grouped(from_beside, 0, g).wait()
+                grouped(from_beside.at[:, upper, :], 0, g).wait()
             for i in range(g * span, g * span + span):
                 sums = own_pair[i, upper, :].astype(jnp.float32)
                 sums = sums + from_beside[i, upper, :].astype(jnp.float32)
                 to_cross[i] = sums.astype(jnp.bfloat16)
                 cross(i).start()
 
-        for p in range(pieces):
-            for s in (1, 0):
-                there = (lower, upper)[s]
+        for s in (1, 0):
+            there = (lower, upper)[s]
+            for p in range(pieces):
                 with scope(f"w_bx{s}{p}"):
                     back_x(s, p).wait_recv()
                 both = keep[p, there, :] + first_in[p, there, :].astype(jnp.float32)
                 second_out[p, there, :] = both.astype(jnp.bfloat16)
                 back_z(s, p).start()
-            for g in range(groups):
-                if p == pieces - groups + g:
-                    pl.when(is_inner)(functools.partial(merge, g))
-                if p == 1 + 2 * g:
-                    pl.when(is_outer)(functools.partial(merge, g))
+            if s == 1:
+                for g in range(groups):
+                    merge(g)
+        with scope("w_low"):
+            whole(from_beside.at[:, lower, :], near_recv.at[2, 0]).wait()
         for p in range(pieces):
             if p % span == 0:
                 with scope(f"w_xA{p}"):
@@ -507,9 +516,9 @@
             dma((3,)),
             dma((6,)),
             dma((2, max(batches, pieces))),
-            dma,
+            dma((2,)),
             dma((pieces,)),
-            dma((2, 2)),
+            dma((3, 2)),
             dma,
         ],
         compiler_params=pltpu.CompilerParams(

time: 27.9 us -> 26.4 us (0.946)
  the two profiles are of different devices: /device:TPU:0 before, /device:TPU:9 now
where the time goes in v7:
time: 26.4 us; the launch traced here: 26.3 us
  Pallas kernels  25.6 us (97%)
  local copies, waits for them, and re-layouts  0.68 us (3%)
    pallas_call x1, Pallas kernels, dense_layer(): pl.pallas_call(dense_kernel, out_shape=pltpu.VMEM(tokens.shape, tokens.dt...  25.6 us
    unnamed x1, local copies, waits for them, and re-layouts  0.68 us

profile of v7, /device:TPU:9, one launch (start us, length us, event | category | flops | bytes accessed | tf_op | source)
XLA Modules:
  0.0 26.3 jit_solution(15180244572475765473)
XLA Ops:
  0.0 25.6 %shard_map.73 = bf16[64,1536]{1,0:T(8,128)(2,1)S(1)} custom-call(bf16[64,1536]{1,0:T(8,128)(2,1)} %tokens_ref.1, f32[1536]{0:T(1024)} %gain_ref.1, s32[4,64]{1,0:T(4,128)} %bitcast.2, f32[4,64]{1,0:T(4,128)} %bitcast.3, bf16[1,1536,384]{2,1,0:T(8,128)(2,1)} %gate_ref.1, bf16[1,1536,384]{2,1,0:T(8,128)(2,1)} %up_ref.1, bf16[1,384,1536]{2,1,0:T(8,128)(2,1)} %down_ref.1), custom_call_target="tpu_custom_call" | custom-call | tf_op jit(solution)/shard_map/pallas_call | solution.py:492
  25.6 0.7 %copy.9 = bf16[64,1536]{1,0:T(8,128)(2,1)} copy(bf16[64,1536]{1,0:T(8,128)(2,1)S(1)} %shard_map.73) | data formatting | bytes 393216

commit v8 on v7

--- a/solution.py
+++ b/solution.py
@@ -32,7 +32,9 @@
     wd,
     own,
     slots,
-    keep,
+    far_rows,
+    far_out,
+    far_in,
     first_out,
     first_in,
     second_out,
@@ -81,7 +83,7 @@
     batches = rows // 16
     groups = near_recv.shape[1]
     batch = rows // batches
-    pieces, _, width = keep.shape
+    pieces, _, width = far_out.shape
     scope = jax.named_scope
 
     barrier = pltpu.get_barrier_semaphore()
@@ -175,8 +177,7 @@
         loads[i].wait()
         swaps[i].wait_recv()
 
-    def hidden_of(first, count, fresh):
-        block = slots[pl.ds(first, count)].reshape(count * rows, features)
+    def hidden_of(block, fresh):
         if fresh:
             with scope("w_wg"):
                 ready(0)
@@ -190,6 +191,9 @@
             with scope("w_wd"):
                 ready(2)
         return value
+
+    def stacked(ref, first):
+        return ref[pl.ds(first, 2)].reshape(2 * rows, features)
 
     def down(hidden, p):
         return jnp.dot(hidden, wd[:, part(p)], preferred_element_type=jnp.float32)
@@ -281,7 +285,7 @@
             )
             return column(own_line)
 
-        hidden = hidden_of(0, 2, True)
+        hidden = hidden_of(stacked(slots, 0), True)
         with scope("w_line"):
             whole(line_in, done_recv.at[0]).wait()
         own_share = share(line_out[...])
@@ -298,6 +302,19 @@
         for p in range(pieces):
             hand_pair(p).start()
 
+        def far_products():
+            with scope("w_far"):
+                whole(far_rows, rest_recv.at[1]).wait()
+            value = hidden_of(stacked(far_rows, 0), False)
+            for p in range(pieces):
+                far_out[p] = down(value, p).astype(jnp.bfloat16)
+            for p in range(pieces):
+                remote(
+                    far_out.at[p], far_in.at[p], sent.at[6], near_recv.at[3, 0], sibling
+                ).start()
+
+        pl.when(is_inner)(far_products)
+
         @pl.when(is_inner)
         def _():
             for q in range(batches):
@@ -306,7 +323,7 @@
 
         with scope("w_D"):
             whole(slots.at[3], rest_recv.at[0]).wait()
-        hidden = hidden_of(2, 2, False)
+        hidden = hidden_of(stacked(slots, 2), False)
         scales = jnp.concatenate([shares[1], shares[2]], axis=0)
         for batch_of in batched:
             for p in batch_of:
@@ -314,7 +331,9 @@
             for p in batch_of:
                 along(p, upper, near_recv.at[0, group(p)]).start()
         for p in range(pieces):
-            along(p, lower, near_recv.at[2, 0]).start()
+            along(p, lower, near_recv.at[2, group(p)]).start()
+        pl.when(is_outer)(far_products)
+        whole(far_out, sent.at[6]).wait()
         whole(line_in, sent.at[5]).wait()
 
         @pl.when(is_outer)
@@ -349,6 +368,12 @@
 
         def arrived(s, q):
             return spread(s, q, slots.at[s], beside, spread_recv.at[s, q])
+
+        def pass_on(s, q):
+            return remote(
+                slots.at[s, rows_of(q), :], far_rows.at[s, rows_of(q), :], sent.at[0],
+                rest_recv.at[1], sibling,
+            )
 
         def sideways(s, q):
             return spread(3 - s, q, slots.at[s], across, rest_recv.at[s])
@@ -401,24 +426,25 @@
                 arrived(s, q).start()
 
             sideways(s, q).start()
+            pass_on(s, q).start()
         with scope("w_G1"):
             whole(slots.at[2], rest_recv.at[1]).wait()
-        hidden = hidden_of(0, 3, True)
+        hidden = hidden_of(slots[2], True)
         for batch_of in batched:
             for p in batch_of:
-                first_out[p, upper, :] = down(hidden[2 * rows :], p).astype(jnp.bfloat16)
+                first_out[p, upper, :] = down(hidden, p).astype(jnp.bfloat16)
             for p in batch_of:
                 back_x(1, p).start()
         with scope("w_G0"):
             whole(slots.at[3], rest_recv.at[0]).wait()
-        late_hidden = hidden_of(3, 1, False)
+        late_hidden = hidden_of(slots[3], False)
         for batch_of in batched:
             for p in batch_of:
                 first_out[p, lower, :] = down(late_hidden, p).astype(jnp.bfloat16)
             for p in batch_of:
                 back_x(0, p).start()
-        for p in range(pieces):
-            keep[p] = down(hidden[: 2 * rows], p)
+        with scope("w_far"):
+            whole(far_in, near_recv.at[3, 0]).wait()
         span = pieces // groups
 
         def merge(g):
@@ -437,18 +463,22 @@
             for p in range(pieces):
                 with scope(f"w_bx{s}{p}"):
                     back_x(s, p).wait_recv()
-                both = keep[p, there, :] + first_in[p, there, :].astype(jnp.float32)
+                both = far_in[p, there, :].astype(jnp.float32)
+                both = both + first_in[p, there, :].astype(jnp.float32)
                 second_out[p, there, :] = both.astype(jnp.bfloat16)
                 back_z(s, p).start()
-            if s == 1:
+
+            @pl.when((place == 0) == (s == 1))
+            def _():
                 for g in range(groups):
                     merge(g)
-        with scope("w_low"):
-            whole(from_beside.at[:, lower, :], near_recv.at[2, 0]).wait()
+
         for p in range(pieces):
             if p % span == 0:
                 with scope(f"w_xA{p}"):
                     grouped(from_across, 1, group(p)).wait()
+                with scope(f"w_low{p}"):
+                    grouped(from_beside.at[:, lower, :], 2, group(p)).wait()
             total = held[:, part(p)].astype(jnp.float32)
             total = total + own_pair[p, lower, :].astype(jnp.float32)
             total = total + from_beside[p, lower, :].astype(jnp.float32)
@@ -459,16 +489,16 @@
                 total = total + shares[s] * second_in[p, (lower, upper)[s], :].astype(jnp.float32)
             out_ref[:, part(p)] = total.astype(jnp.bfloat16)
             give(p).start()
-        whole(keep, sent.at[1]).wait()
+        whole(slots, sent.at[1]).wait()
         whole(to_cross, sent.at[2]).wait()
 
         @pl.when(is_inner)
         def _():
-            blocks_sent(7)
+            blocks_sent(9)
 
         @pl.when(is_outer)
         def _():
-            blocks_sent(5)
+            blocks_sent(7)
 
         swaps_sent()
         with scope("w_end"):
@@ -504,9 +534,9 @@
             pltpu.VMEM((units, features), half),
             pltpu.VMEM((rows, features), half),
             pltpu.VMEM((4, rows, features), half),
-            pltpu.VMEM((pieces, 2 * rows, width), jnp.float32),
+            pltpu.VMEM((2, rows, features), half),
         ]
-        + [travel] * 6
+        + [travel] * 8
         + [single] * 2
         + [
             pltpu.VMEM(weights.shape, jnp.float32),
@@ -514,11 +544,11 @@
             dma((4,)),
             dma((3,)),
             dma((3,)),
-            dma((6,)),
+            dma((7,)),
             dma((2, max(batches, pieces))),
             dma((2,)),
             dma((pieces,)),
-            dma((3, 2)),
+            dma((4, 2)),
             dma,
         ],
         compiler_params=pltpu.CompilerParams(

time: 26.4 us -> 26.2 us (level)
  the two profiles are of different devices: /device:TPU:9 before, /device:TPU:0 now
where the time goes in v8:
time: 26.2 us; the launch traced here: 26.1 us
  Pallas kernels  25.4 us (97%)
  local copies, waits for them, and re-layouts  0.68 us (3%)
    pallas_call x1, Pallas kernels, dense_layer(): pl.pallas_call(dense_kernel, out_shape=pltpu.VMEM(tokens.shape, tokens.dt...  25.4 us
    unnamed x1, local copies, waits for them, and re-layouts  0.68 us

profile of v8, /device:TPU:0, one launch (start us, length us, event | category | flops | bytes accessed | tf_op | source)
XLA Modules:
  0.0 26.1 jit_solution(214300634132262474)
XLA Ops:
  0.0 25.4 %shard_map.73 = bf16[64,1536]{1,0:T(8,128)(2,1)S(1)} custom-call(bf16[64,1536]{1,0:T(8,128)(2,1)} %tokens_ref.1, f32[1536]{0:T(1024)} %gain_ref.1, s32[4,64]{1,0:T(4,128)} %bitcast.2, f32[4,64]{1,0:T(4,128)} %bitcast.3, bf16[1,1536,384]{2,1,0:T(8,128)(2,1)} %gate_ref.1, bf16[1,1536,384]{2,1,0:T(8,128)(2,1)} %up_ref.1, bf16[1,384,1536]{2,1,0:T(8,128)(2,1)} %down_ref.1), custom_call_target="tpu_custom_call" | custom-call | tf_op jit(solution)/shard_map/pallas_call | solution.py:522
  25.4 0.7 %copy.9 = bf16[64,1536]{1,0:T(8,128)(2,1)} copy(bf16[64,1536]{1,0:T(8,128)(2,1)S(1)} %shard_map.73) | data formatting | bytes 393216

commit v9 on v8

--- a/solution.py
+++ b/solution.py
@@ -47,7 +47,6 @@
     line_in,
     small_sem,
     load_sem,
-    swap_recv,
     sent,
     spread_recv,
     rest_recv,
@@ -142,7 +141,7 @@
         )
 
     swaps = [
-        remote(src, dst(1), sent.at[3 + i // 2], swap_recv.at[i], sibling)
+        remote(src, dst(1), sent.at[3 + i // 2], load_sem.at[i], sibling)
         for i, (src, dst) in enumerate(pairs)
     ]
 
@@ -174,8 +173,7 @@
         return jnp.sum(jnp.where(spot_ids == lane_ids, line, 0.0), axis=1, keepdims=True)
 
     def ready(i):
-        loads[i].wait()
-        swaps[i].wait_recv()
+        whole((wg, wu, wd)[i], load_sem.at[i]).wait()
 
     def hidden_of(block, fresh):
         if fresh:
@@ -198,8 +196,9 @@
     def down(hidden, p):
         return jnp.dot(hidden, wd[:, part(p)], preferred_element_type=jnp.float32)
 
-    def give(p):
-        there = out_ref.at[:, part(p)]
+    def give(g):
+        span = features // groups
+        there = out_ref.at[:, pl.ds(g * span, span)]
         return remote(there, there, sent.at[5], done_recv.at[1], sibling)
 
     def whole(ref, sem):
@@ -488,7 +487,8 @@
             for s in range(2):
                 total = total + shares[s] * second_in[p, (lower, upper)[s], :].astype(jnp.float32)
             out_ref[:, part(p)] = total.astype(jnp.bfloat16)
-            give(p).start()
+            if (p + 1) % span == 0:
+                give(group(p)).start()
         whole(slots, sent.at[1]).wait()
         whole(to_cross, sent.at[2]).wait()
 
@@ -543,7 +543,6 @@
             pltpu.VMEM((3, *weights.shape), jnp.float32),
             dma((4,)),
             dma((3,)),
-            dma((3,)),
             dma((7,)),
             dma((2, max(batches, pieces))),
             dma((2,)),

time: 26.2 us -> 26.3 us (level)
  no operation moved by 1% of the time
where the time goes in v9:
time: 26.3 us; the launch traced here: 26.1 us
  Pallas kernels  25.4 us (97%)
  local copies, waits for them, and re-layouts  0.68 us (3%)
    pallas_call x1, Pallas kernels, dense_layer(): pl.pallas_call(dense_kernel, out_shape=pltpu.VMEM(tokens.shape, tokens.dt...  25.4 us
    unnamed x1, local copies, waits for them, and re-layouts  0.68 us

profile of v9, /device:TPU:0, one launch (start us, length us, event | category | flops | bytes accessed | tf_op | source)
XLA Modules:
  0.0 26.1 jit_solution(7052858187046002860)
XLA Ops:
  0.0 25.4 %shard_map.73 = bf16[64,1536]{1,0:T(8,128)(2,1)S(1)} custom-call(bf16[64,1536]{1,0:T(8,128)(2,1)} %tokens_ref.1, f32[1536]{0:T(1024)} %gain_ref.1, s32[4,64]{1,0:T(4,128)} %bitcast.2, f32[4,64]{1,0:T(4,128)} %bitcast.3, bf16[1,1536,384]{2,1,0:T(8,128)(2,1)} %gate_ref.1, bf16[1,1536,384]{2,1,0:T(8,128)(2,1)} %up_ref.1, bf16[1,384,1536]{2,1,0:T(8,128)(2,1)} %down_ref.1), custom_call_target="tpu_custom_call" | custom-call | tf_op jit(solution)/shard_map/pallas_call | solution.py:522
  25.4 0.7 %copy.9 = bf16[64,1536]{1,0:T(8,128)(2,1)} copy(bf16[64,1536]{1,0:T(8,128)(2,1)S(1)} %shard_map.73) | data formatting | bytes 393216

commit v10 on v9

--- a/solution.py
+++ b/solution.py
@@ -110,7 +110,7 @@
             greet(far)
 
     smalls = [
-        pltpu.make_async_copy(src, dst, small_sem.at[i])
+        pltpu.make_async_copy(src, dst, small_sem.at[min(i, 2)])
         for i, (src, dst) in enumerate(
             (
                 (tokens_ref, held),
@@ -253,8 +253,7 @@
             )
 
         slots[0] = normed()
-        smalls[2].wait()
-        smalls[3].wait()
+        whole(line_in.at[pl.ds(0, 2)], small_sem.at[2]).wait()
         for spot in range(spots):
             line_out[spot : spot + 1, :] = line_of(spot)
         with scope("w_bar"):
@@ -309,7 +308,7 @@
                 far_out[p] = down(value, p).astype(jnp.bfloat16)
             for p in range(pieces):
                 remote(
-                    far_out.at[p], far_in.at[p], sent.at[6], near_recv.at[3, 0], sibling
+                    far_out.at[p], far_in.at[p], sent.at[6], sent.at[6], sibling
                 ).start()
 
         pl.when(is_inner)(far_products)
@@ -389,12 +388,12 @@
                 second_out.at[p, (lower, upper)[s], :],
                 second_in.at[p, pl.ds(pl.multiple_of(my_far_slot * rows, rows), rows), :],
                 sent.at[1],
-                done_recv.at[p],
+                done_recv.at[p // 2],
                 far[s],
             )
 
         def came_z(p):
-            return whole(second_in.at[p], done_recv.at[p])
+            return whole(second_in.at[pl.ds(p, 2)], done_recv.at[p // 2])
 
         def cross(p):
             return remote(
@@ -413,8 +412,7 @@
             near_z(q).start()
         for swap in swaps:
             swap.start()
-        smalls[2].wait()
-        smalls[3].wait()
+        whole(line_in.at[pl.ds(0, 2)], small_sem.at[2]).wait()
         shares = [column(line_of(spot)) for spot in far_spots]
         for s, q in [(1, q) for q in range(batches)] + [(0, q) for q in range(batches)]:
             with scope(f"w_F{s}{q}"):
@@ -443,7 +441,7 @@
             for p in batch_of:
                 back_x(0, p).start()
         with scope("w_far"):
-            whole(far_in, near_recv.at[3, 0]).wait()
+            whole(far_in, sent.at[6]).wait()
         span = pieces // groups
 
         def merge(g):
@@ -482,8 +480,9 @@
             total = total + own_pair[p, lower, :].astype(jnp.float32)
             total = total + from_beside[p, lower, :].astype(jnp.float32)
             total = total + from_across[p].astype(jnp.float32)
-            with scope(f"w_bz{p}"):
-                came_z(p).wait()
+            if p % 2 == 0:
+                with scope(f"w_bz{p}"):
+                    came_z(p).wait()
             for s in range(2):
                 total = total + shares[s] * second_in[p, (lower, upper)[s], :].astype(jnp.float32)
             out_ref[:, part(p)] = total.astype(jnp.bfloat16)
@@ -541,13 +540,13 @@
         + [
             pltpu.VMEM(weights.shape, jnp.float32),
             pltpu.VMEM((3, *weights.shape), jnp.float32),
-            dma((4,)),
+            dma((3,)),
             dma((3,)),
             dma((7,)),
             dma((2, max(batches, pieces))),
             dma((2,)),
-            dma((pieces,)),
-            dma((4, 2)),
+            dma((pieces // 2,)),
+            dma((3, 2)),
             dma,
         ],
         compiler_params=pltpu.CompilerParams(

time: 26.3 us -> 26.2 us (level)
  no operation moved by 1% of the time
where the time goes in v10:
time: 26.2 us; the launch traced here: 26.1 us
  Pallas kernels  25.4 us (97%)
  local copies, waits for them, and re-layouts  0.68 us (3%)
    pallas_call x1, Pallas kernels, dense_layer(): pl.pallas_call(dense_kernel, out_shape=pltpu.VMEM(tokens.shape, tokens.dt...  25.4 us
    unnamed x1, local copies, waits for them, and re-layouts  0.68 us

profile of v10, /device:TPU:0, one launch (start us, length us, event | category | flops | bytes accessed | tf_op | source)
XLA Modules:
  0.0 26.1 jit_solution(12976703092380042542)
XLA Ops:
  0.0 25.4 %shard_map.73 = bf16[64,1536]{1,0:T(8,128)(2,1)S(1)} custom-call(bf16[64,1536]{1,0:T(8,128)(2,1)} %tokens_ref.1, f32[1536]{0:T(1024)} %gain_ref.1, s32[4,64]{1,0:T(4,128)} %bitcast.2, f32[4,64]{1,0:T(4,128)} %bitcast.3, bf16[1,1536,384]{2,1,0:T(8,128)(2,1)} %gate_ref.1, bf16[1,1536,384]{2,1,0:T(8,128)(2,1)} %up_ref.1, bf16[1,384,1536]{2,1,0:T(8,128)(2,1)} %down_ref.1), custom_call_target="tpu_custom_call" | custom-call | tf_op jit(solution)/shard_map/pallas_call | solution.py:521
  25.4 0.7 %copy.9 = bf16[64,1536]{1,0:T(8,128)(2,1)} copy(bf16[64,1536]{1,0:T(8,128)(2,1)S(1)} %shard_map.73) | data formatting | bytes 393216
